TPU v7x, 256 devices: a whole 4x4x8 slice. The times are simulated.
256 devices in a mesh: ctg: 32 (over x, y, core), br: 8 (over z).
Axes of the slice: x: 4, y: 4, z: 8, core: 2. Of those that a mesh axis runs over, the one named last changes fastest.
Arguments:
- base_vm: float32 [10240], P(('ctg', 'br')), may hold values from 0.95 to 1.05
- base_va: float32 [10240], P(('ctg', 'br')), may hold values from -0.6 to 0.6
- delta_state: float32 [256, 2, 10240], P('ctg', None, 'br'), may hold values from -0.18 to 0.18
- multipliers: float32 [256, 2, 10240], P('ctg', None, 'br'), may hold values from -6 to 6
- net_inj: float32 [256, 2, 10240], P('ctg', None, 'br'), may hold values from -6 to 6
- ang_grad: float32 [256, 10240], P('ctg', 'br'), may hold values from -6 to 6
- from_bus: int32 [13312], P('br'), may hold values from 0 to 10239
- to_bus: int32 [13312], P('br'), may hold values from 0 to 10239
- status: int32 [256, 13312], P('ctg', 'br'), may hold values 0 or 1
- conduct: float32 [13312], P('br'), may hold values from 1 to 5
- suscept: float32 [13312], P('br'), may hold values from -15 to -5
- charging: float32 [13312], P('br'), may hold values from 0.1 to 0.6
- rating: float32 [13312], P('br'), may hold values from 1 to 3
- slack: float32 [256, 13312], P('ctg', 'br'), may hold values from 0.05 to 2
- zdual: float32 [256, 13312], P('ctg', 'br'), may hold values from 0.05 to 2
Outputs:
- mismatch: float32 [256, 2, 10240], P('ctg', None, 'br')
- dual_res: float32 [256, 10240], P('ctg', 'br')
- limit_res: float32 [256, 13312], P('ctg', 'br')
- ctg_norms: float32 [256, 4], P('ctg')
- total_norms: float32 [4], replicated
All inputs are finite; a program needn't handle non-finite values. No bound on the sum of `status` on one device may be relied on, other than what follows from the above.
Results may differ from a plain program's by a relative error of at most 0.0003.
Values sent between devices are 32-bit elements; how exact they have to be, the bound alone decides.
No kernel may reach another device: no remote copies, remote signals or barrier semaphores. Data moves between devices by JAX's collectives and lax.ppermute only.
A program may use at most 64 MiB of HBM per device.

v0:
```python
import math

import jax
import jax.numpy as jnp
from jax import lax
from jax.sharding import PartitionSpec as P


def turned_gather(arrays, axis, dims):
    turned = [jnp.moveaxis(a, dim, 0) for a, dim in zip(arrays, dims)]
    widths = [t[0].size for t in turned]
    both = jnp.concatenate([t.reshape(-1, w) for t, w in zip(turned, widths)], axis=1)
    whole = lax.all_gather(both, axis, axis=0, tiled=True)
    pieces = jnp.split(whole, [sum(widths[:k]) for k in range(1, len(widths))], axis=1)
    return tuple(
        (
            jnp.moveaxis(b.reshape(-1, *t.shape[1:]), 0, dim)
            for b, t, dim in zip(pieces, turned, dims)
        )
    )


def in_one_piece(arrays, axis, dim, along):
    both = jnp.concatenate(arrays, axis=along)
    whole, at, finished = (lax.all_gather(both, axis, axis=dim, tiled=True), 0, [])
    for a in arrays:
        finished.append(lax.slice_in_dim(whole, at, at + a.shape[along], axis=along))
        at += a.shape[along]
    return tuple(finished)


def in_blocks(array, dim, peers):
    shape = array.shape
    pieces = array.reshape(*shape[:dim], peers, shape[dim] // peers, *shape[dim + 1 :])
    return jnp.moveaxis(pieces, dim, 0)


def summed_on_arrival(array, axis, dim):
    peers = lax.axis_size(axis)
    pieces = lax.all_to_all(in_blocks(array, dim, peers), axis, 0, 0, tiled=True)
    return jnp.sum(pieces, axis=0)


def sent_to_all(array, axis):
    copies = jnp.broadcast_to(array, (lax.axis_size(axis), *array.shape))
    return lax.all_to_all(copies, axis, split_axis=0, concat_axis=0, tiled=True)


def over_copies(array, axis):
    everything = sent_to_all(array, axis)
    return jnp.sum(everything, axis=0)


def in_one(arrays, axis):
    ends = [0]
    for a in arrays:
        ends.append(ends[-1] + a.size)
    subtotal = over_copies(jnp.concatenate([a.ravel() for a in arrays]), axis)
    return tuple((subtotal[b:e].reshape(a.shape) for a, b, e in zip(arrays, ends, ends[1:])))


def block_size(span_total, other_side):
    limit = max(128, (1 << 23) // other_side)
    power = 1 << limit.bit_length() - 1
    return math.gcd(span_total, min(1024, power))


def select_cols(values, index_list):
    row_count, bus_count = values.shape
    col_count = index_list.shape[0]
    span_cols = block_size(bus_count, col_count)
    block_count = bus_count // span_cols
    tiles = values.reshape(row_count, block_count, span_cols).transpose(1, 0, 2)

    def add_block(running, item):
        segment, number = item
        labels = number * span_cols + lax.iota(jnp.int32, span_cols)
        onehot = (labels[:, None] == index_list[None, :]).astype(jnp.float32)
        running = running + jnp.dot(
            segment, onehot, precision=lax.Precision.HIGHEST, preferred_element_type=jnp.float32
        )
        return (running, None)

    start_zero = jnp.zeros((row_count, col_count), jnp.float32)
    numbers = jnp.arange(block_count, dtype=jnp.int32)
    result, _ = lax.scan(add_block, start_zero, (tiles, numbers))
    return result


def spread_rows(values, index_list, bus_count):
    row_count, col_count = values.shape
    span_cols = block_size(bus_count, col_count)
    block_count = bus_count // span_cols

    def one_block(carry, number):
        labels = number * span_cols + lax.iota(jnp.int32, span_cols)
        onehot = (index_list[:, None] == labels[None, :]).astype(jnp.float32)
        piece_sum = jnp.dot(
            values, onehot, precision=lax.Precision.HIGHEST, preferred_element_type=jnp.float32
        )
        return (carry, piece_sum)

    numbers = jnp.arange(block_count, dtype=jnp.int32)
    _, pieces = lax.scan(one_block, jnp.int32(0), numbers)
    return pieces.transpose(1, 0, 2).reshape(row_count, bus_count)


def branch_flows(
    volt_mag, volt_ang, mult_p, mult_q, from_idx, to_idx, conduct, suscept, charging, in_service
):
    scen_count = volt_mag.shape[0]
    stacked = jnp.concatenate([volt_mag, volt_ang, mult_p, mult_q], 0)
    at_from_end = select_cols(stacked, from_idx)
    at_to_end = select_cols(stacked, to_idx)
    volt_from = at_from_end[:scen_count]
    volt_to = at_to_end[:scen_count]
    angle_diff = at_from_end[scen_count : 2 * scen_count] - at_to_end[scen_count : 2 * scen_count]
    mp_from = at_from_end[2 * scen_count : 3 * scen_count]
    mq_from = at_from_end[3 * scen_count :]
    mp_to = at_to_end[2 * scen_count : 3 * scen_count]
    mq_to = at_to_end[3 * scen_count :]
    cos_diff = jnp.cos(angle_diff)
    sin_diff = jnp.sin(angle_diff)
    volt_prod = volt_from * volt_to
    p_from = conduct * volt_from * volt_from - volt_prod * (conduct * cos_diff + suscept * sin_diff)
    q_from = -(suscept + charging) * volt_from * volt_from - volt_prod * (
        conduct * sin_diff - suscept * cos_diff
    )
    p_to = conduct * volt_to * volt_to - volt_prod * (conduct * cos_diff - suscept * sin_diff)
    q_to = -(suscept + charging) * volt_to * volt_to + volt_prod * (
        conduct * sin_diff + suscept * cos_diff
    )
    flow_dual = volt_prod * (
        mp_from * (conduct * sin_diff - suscept * cos_diff)
        - mq_from * (conduct * cos_diff + suscept * sin_diff)
        + mp_to * (conduct * sin_diff + suscept * cos_diff)
        + mq_to * (conduct * cos_diff - suscept * sin_diff)
    )
    at_from = jnp.stack([p_from, q_from, flow_dual], 1) * in_service[:, None, :]
    at_to = jnp.stack([p_to, q_to, -flow_dual], 1) * in_service[:, None, :]
    return (at_from, at_to)


def sum_at_buses(from_vals, to_vals, from_idx, to_idx, offset, bus_count):
    scen_count = from_vals.shape[0]
    both_vals = jnp.concatenate([from_vals, to_vals], 2).reshape(scen_count * 3, -1)
    both_idx = jnp.concatenate([from_idx, to_idx], 0) - offset
    summed = spread_rows(both_vals, both_idx, bus_count)
    return summed.reshape(scen_count, 3, bus_count)


def per_device(
    base_vm,
    base_va,
    delta_state,
    multipliers,
    net_inj,
    ang_grad,
    from_bus,
    to_bus,
    status,
    conduct,
    suscept,
    charging,
    rating,
    slack,
    zdual,
):
    full_vm, full_va = turned_gather((base_vm, base_va), ("ctg", "br"), (0, 0))
    shifts, duals_all = in_one_piece((delta_state, multipliers), "br", 2, 0)
    volt_mag = full_vm[None, :] + shifts[:, 0]
    volt_ang = full_va[None, :] + shifts[:, 1]
    in_service = status.astype(jnp.float32)
    at_from, at_to = branch_flows(
        volt_mag,
        volt_ang,
        duals_all[:, 0],
        duals_all[:, 1],
        from_bus,
        to_bus,
        conduct,
        suscept,
        charging,
        in_service,
    )
    limit_res = in_service * (
        at_from[:, 0] * at_from[:, 0] + at_from[:, 1] * at_from[:, 1] + slack - rating * rating
    )
    complement = in_service * (zdual * slack - 0.01)
    limit_part = jnp.sum(limit_res * limit_res, axis=1)
    comp_part = jnp.sum(complement * complement, axis=1)
    bus_terms = sum_at_buses(at_from, at_to, from_bus, to_bus, 0, shifts.shape[2])
    summed = summed_on_arrival(bus_terms, "br", 2)
    mismatch = summed[:, :2] - net_inj
    dual_res = summed[:, 2] + ang_grad
    mis_part = jnp.sum(mismatch * mismatch, axis=(1, 2))
    dual_part = jnp.sum(dual_res * dual_res, axis=1)
    mis_sq, dual_sq, limit_sq, comp_sq = in_one((mis_part, dual_part, limit_part, comp_part), "br")
    squares = jnp.stack([mis_sq, dual_sq, limit_sq, comp_sq], 1)
    ctg_norms = jnp.sqrt(squares)
    totals = over_copies(jnp.sum(squares, axis=0), "ctg")
    total_norms = jnp.sqrt(totals / (delta_state.shape[0] * lax.axis_size("ctg")))
    return (mismatch, dual_res, limit_res, ctg_norms, total_norms)


def solution(mesh):
    placed = (
        P(("ctg", "br")),
        P(("ctg", "br")),
        P("ctg", None, "br"),
        P("ctg", None, "br"),
        P("ctg", None, "br"),
        P("ctg", "br"),
        P("br"),
        P("br"),
        P("ctg", "br"),
        P("br"),
        P("br"),
        P("br"),
        P("br"),
        P("ctg", "br"),
        P("ctg", "br"),
    )
    return jax.shard_map(
        per_device,
        mesh=mesh,
        in_specs=placed,
        out_specs=(P("ctg", None, "br"), P("ctg", "br"), P("ctg", "br"), P("ctg", None), P()),
        check_vma=False,
    )
```

profile of v0, /device:TPU:1, one launch (start us, length us, event | category | flops | bytes accessed | tf_op | source)
XLA Modules:
  0.0 281.0 jit_solution(867481893369995764)
XLA Ops:
  10.5 67.2 %all-gather = f32[256,40,2]{1,2,0:T(2,128)S(1)} all-gather(f32[1,40,2]{1,2,0:T(2,128)S(1)} %maximum_bitcast_fusion.1), channel_id=1, replica_groups=mesh['ctg'=32,'br'=8] {'ctg','br'}, dimensions={0}, use_global_device_ids=true | all-gather | bytes 82240 | tf_op jit(solution)/shard_map/all_gather | solution.py:13
  79.9 36.7 %while.34 = (s32[]{:T(128)}, f32[32,1664]{1,0:T(8,128)S(1)}, f32[10,32,1024]{2,1,0:T(8,128)S(1)}, s32[10]{0:T(128)S(1)}, s32[1664]{0:T(1024)S(1)}, /*index=5*/s32[]{:T(128)}, s32[1]{0:T(128)}, s32[]{:T(128)}) while((s32[]{:T(128)}, f32[32,1664]{1,0:T(8,128)S(1)}, f32[10,32,1024]{2,1,0:T(8,128)S(1)}, s32[10]{0:T(128)S(1)}, ...), condition=%wide.region_3.4_spmd.clone, body=%wide.region_2.3_spmd.clone.sunk | while | flops 656122880 | bytes 573567 | solution.py:86
  84.8 2.4 fusion.71
  88.5 2.4 fusion.71
  92.2 2.4 fusion.71
  116.6 36.7 %while.33 = (s32[]{:T(128)}, f32[32,1664]{1,0:T(8,128)S(1)}, f32[10,32,1024]{2,1,0:T(8,128)S(1)}, s32[10]{0:T(128)S(1)}, s32[1664]{0:T(1024)S(1)}, /*index=5*/s32[]{:T(128)}, s32[1]{0:T(128)}, s32[]{:T(128)}) while((s32[]{:T(128)}, f32[32,1664]{1,0:T(8,128)S(1)}, f32[10,32,1024]{2,1,0:T(8,128)S(1)}, s32[10]{0:T(128)S(1)}, ...), condition=%wide.region_1.2_spmd.clone, body=%wide.region_0.1_spmd.clone.sunk | while | flops 656122880 | bytes 573567 | solution.py:86
  139.9 2.4 fusion.68
  143.6 2.4 fusion.68
  147.3 2.4 fusion.68
  154.0 59.3 %while.32 = (s32[]{:T(128)}, f32[10,24,1024]{2,1,0:T(8,128)}, s32[3328]{0:T(1024)S(1)}, s32[10]{0:T(128)S(1)}, f32[24,3328]{1,0:T(8,128)S(1)}, /*index=5*/s32[]{:T(128)}, s32[1]{0:T(128)}) while((s32[]{:T(128)}, f32[10,24,1024]{2,1,0:T(8,128)}, s32[3328]{0:T(1024)S(1)}, s32[10]{0:T(128)S(1)}, f32[24,3328]{1,0:T(8,128)S(1)}, ...), condition=%wide.region_5.6_spmd, body=%wide.region_4.5_spmd.sunk | while | flops 984876032 | bytes 439913 | solution.py:104
  155.3 4.7 %fusion.65 = f32[10,24,1024]{2,1,0:T(8,128)} fusion(f32[10,24,1024]{2,1,0:T(8,128)} %get-tuple-element.346, s32[]{:T(128)} %get-tuple-element.345, f32[24,3328]{1,0:T(8,128)S(1)} %get-tuple-element.356, s32[1024]{0:T(1024)S(1)} %iota_add_fusion.6, s32[3328]{0:T(1024)S(1)} %get-tuple-element.354), kind=kOutput, calls=%fused_computation.5.clone.1 | convolution fusion | flops 984875008 | bytes 435712 | tf_op jit(solution)/shard_map/while/body/eval_jaxpr/dot_general | solution.py:98
  161.2 4.7 %fusion.65 = f32[10,24,1024]{2,1,0:T(8,128)} fusion(f32[10,24,1024]{2,1,0:T(8,128)} %get-tuple-element.346, s32[]{:T(128)} %get-tuple-element.345, f32[24,3328]{1,0:T(8,128)S(1)} %get-tuple-element.356, s32[1024]{0:T(1024)S(1)} %iota_add_fusion.6, s32[3328]{0:T(1024)S(1)} %get-tuple-element.354), kind=kOutput, calls=%fused_computation.5.clone.1 | convolution fusion | flops 984875008 | bytes 435712 | tf_op jit(solution)/shard_map/while/body/eval_jaxpr/dot_general | solution.py:98
  167.2 4.7 %fusion.65 = f32[10,24,1024]{2,1,0:T(8,128)} fusion(f32[10,24,1024]{2,1,0:T(8,128)} %get-tuple-element.346, s32[]{:T(128)} %get-tuple-element.345, f32[24,3328]{1,0:T(8,128)S(1)} %get-tuple-element.356, s32[1024]{0:T(1024)S(1)} %iota_add_fusion.6, s32[3328]{0:T(1024)S(1)} %get-tuple-element.354), kind=kOutput, calls=%fused_computation.5.clone.1 | convolution fusion | flops 984875008 | bytes 435712 | tf_op jit(solution)/shard_map/while/body/eval_jaxpr/dot_general | solution.py:98
  173.1 4.7 %fusion.65 = f32[10,24,1024]{2,1,0:T(8,128)} fusion(f32[10,24,1024]{2,1,0:T(8,128)} %get-tuple-element.346, s32[]{:T(128)} %get-tuple-element.345, f32[24,3328]{1,0:T(8,128)S(1)} %get-tuple-element.356, s32[1024]{0:T(1024)S(1)} %iota_add_fusion.6, s32[3328]{0:T(1024)S(1)} %get-tuple-element.354), kind=kOutput, calls=%fused_computation.5.clone.1 | convolution fusion | flops 984875008 | bytes 435712 | tf_op jit(solution)/shard_map/while/body/eval_jaxpr/dot_general | solution.py:98
  179.0 4.7 %fusion.65 = f32[10,24,1024]{2,1,0:T(8,128)} fusion(f32[10,24,1024]{2,1,0:T(8,128)} %get-tuple-element.346, s32[]{:T(128)} %get-tuple-element.345, f32[24,3328]{1,0:T(8,128)S(1)} %get-tuple-element.356, s32[1024]{0:T(1024)S(1)} %iota_add_fusion.6, s32[3328]{0:T(1024)S(1)} %get-tuple-element.354), kind=kOutput, calls=%fused_computation.5.clone.1 | convolution fusion | flops 984875008 | bytes 435712 | tf_op jit(solution)/shard_map/while/body/eval_jaxpr/dot_general | solution.py:98
  184.9 4.7 %fusion.65 = f32[10,24,1024]{2,1,0:T(8,128)} fusion(f32[10,24,1024]{2,1,0:T(8,128)} %get-tuple-element.346, s32[]{:T(128)} %get-tuple-element.345, f32[24,3328]{1,0:T(8,128)S(1)} %get-tuple-element.356, s32[1024]{0:T(1024)S(1)} %iota_add_fusion.6, s32[3328]{0:T(1024)S(1)} %get-tuple-element.354), kind=kOutput, calls=%fused_computation.5.clone.1 | convolution fusion | flops 984875008 | bytes 435712 | tf_op jit(solution)/shard_map/while/body/eval_jaxpr/dot_general | solution.py:98
  190.9 4.7 %fusion.65 = f32[10,24,1024]{2,1,0:T(8,128)} fusion(f32[10,24,1024]{2,1,0:T(8,128)} %get-tuple-element.346, s32[]{:T(128)} %get-tuple-element.345, f32[24,3328]{1,0:T(8,128)S(1)} %get-tuple-element.356, s32[1024]{0:T(1024)S(1)} %iota_add_fusion.6, s32[3328]{0:T(1024)S(1)} %get-tuple-element.354), kind=kOutput, calls=%fused_computation.5.clone.1 | convolution fusion | flops 984875008 | bytes 435712 | tf_op jit(solution)/shard_map/while/body/eval_jaxpr/dot_general | solution.py:98
  196.8 4.7 %fusion.65 = f32[10,24,1024]{2,1,0:T(8,128)} fusion(f32[10,24,1024]{2,1,0:T(8,128)} %get-tuple-element.346, s32[]{:T(128)} %get-tuple-element.345, f32[24,3328]{1,0:T(8,128)S(1)} %get-tuple-element.356, s32[1024]{0:T(1024)S(1)} %iota_add_fusion.6, s32[3328]{0:T(1024)S(1)} %get-tuple-element.354), kind=kOutput, calls=%fused_computation.5.clone.1 | convolution fusion | flops 984875008 | bytes 435712 | tf_op jit(solution)/shard_map/while/body/eval_jaxpr/dot_general | solution.py:98
  202.7 4.7 %fusion.65 = f32[10,24,1024]{2,1,0:T(8,128)} fusion(f32[10,24,1024]{2,1,0:T(8,128)} %get-tuple-element.346, s32[]{:T(128)} %get-tuple-element.345, f32[24,3328]{1,0:T(8,128)S(1)} %get-tuple-element.356, s32[1024]{0:T(1024)S(1)} %iota_add_fusion.6, s32[3328]{0:T(1024)S(1)} %get-tuple-element.354), kind=kOutput, calls=%fused_computation.5.clone.1 | convolution fusion | flops 984875008 | bytes 435712 | tf_op jit(solution)/shard_map/while/body/eval_jaxpr/dot_general | solution.py:98
  208.7 4.7 %fusion.65 = f32[10,24,1024]{2,1,0:T(8,128)} fusion(f32[10,24,1024]{2,1,0:T(8,128)} %get-tuple-element.346, s32[]{:T(128)} %get-tuple-element.345, f32[24,3328]{1,0:T(8,128)S(1)} %get-tuple-element.356, s32[1024]{0:T(1024)S(1)} %iota_add_fusion.6, s32[3328]{0:T(1024)S(1)} %get-tuple-element.354), kind=kOutput, calls=%fused_computation.5.clone.1 | convolution fusion | flops 984875008 | bytes 435712 | tf_op jit(solution)/shard_map/while/body/eval_jaxpr/dot_general | solution.py:98
  216.6 4.0 %all-to-all-start = ((f32[8,8,3,1280]{3,1,2,0:T(8,128)}), f32[8,8,3,1280]{3,1,2,0:T(8,128)S(1)}, u32[]{:S(2)}, u32[]{:S(2)}) async-start(f32[8,8,3,1280]{3,1,2,0:T(8,128)} %copy.60), calls=%async_computation | async-start | bytes 1966080 | tf_op jit(solution)/shard_map/all_to_all | solution.py:40
  221.5 24.0 %all-to-all-done = f32[8,8,3,1280]{3,1,2,0:T(8,128)S(1)} async-done(((f32[8,8,3,1280]{3,1,2,0:T(8,128)}), f32[8,8,3,1280]{3,1,2,0:T(8,128)S(1)}, u32[]{:S(2)}, u32[]{:S(2)}) %all-to-all-start) | async-done | bytes 983072 | tf_op jit(solution)/shard_map/all_to_all | solution.py:40
  247.1 8.9 %all_to_all.17 = f32[8,1,32]{2,1,0:T(1,128)S(1)} all-to-all(f32[8,1,32]{2,1,0:T(1,128)S(1)} %broadcast_in_dim.14), channel_id=1, replica_groups=mesh['ctg'=32,'br'=8] {'br'}, dimensions={0} | all-to-all | bytes 2048 | tf_op jit(solution)/shard_map/all_to_all | solution.py:46
  256.9 16.7 %all_to_all.18 = f32[32,1,4]{2,1,0:T(1,128)S(1)} all-to-all(f32[32,1,4]{2,1,0:T(1,128)S(1)} %broadcast_in_dim.15), channel_id=1, replica_groups=mesh['ctg'=32,'br'=8] {'ctg'}, dimensions={0} | all-to-all | bytes 1024 | tf_op jit(solution)/shard_map/all_to_all | solution.py:46
  (145 shorter events, 64.2 us)
Async XLA Ops:
  7.2 71.0 %copy-start = (s32[8,1664]{1,0:T(8,128)S(1)}, s32[8,1664]{1,0:T(8,128)}, u32[]{:S(2)}) copy-start(s32[8,1664]{1,0:T(8,128)} %param.29) | copy-start | bytes 159748
  7.2 71.0 %copy-start.9 = (s32[1664]{0:T(1024)S(1)}, s32[1664]{0:T(1024)}, u32[]{:S(2)}) copy-start(s32[1664]{0:T(1024)} %param.28) | copy-start | bytes 19972
  7.2 71.0 %copy-start.10 = (s32[1664]{0:T(1024)S(1)}, s32[1664]{0:T(1024)}, u32[]{:S(2)}) copy-start(s32[1664]{0:T(1024)} %param.27) | copy-start | bytes 19972
  7.2 71.0 %copy-start.2 = (f32[1664]{0:T(1024)S(1)}, f32[1664]{0:T(1024)}, u32[]{:S(2)}) copy-start(f32[1664]{0:T(1024)} %param.31) | copy-start | bytes 19972
  7.2 71.0 %copy-start.8 = (f32[1664]{0:T(1024)S(1)}, f32[1664]{0:T(1024)}, u32[]{:S(2)}) copy-start(f32[1664]{0:T(1024)} %param.32) | copy-start | bytes 19972
  7.2 71.0 %all-gather.3.cloned.1.call-start = ((), (), s32[]{:S(2)}) async-start(), calls=%async_computation.3 | async-start | bytes 1474560 | tf_op jit(solution)/shard_map/all_gather | solution.py:25
  116.6 36.7 %copy-start.6 = (f32[1664]{0:T(1024)S(1)}, f32[1664]{0:T(1024)}, u32[]{:S(2)}) copy-start(f32[1664]{0:T(1024)} %param.30) | copy-start | bytes 19972
  216.6 4.0 %copy-start.7 = (f32[1664]{0:T(1024)S(1)}, f32[1664]{0:T(1024)}, u32[]{:S(2)}) copy-start(f32[1664]{0:T(1024)} %param.33) | copy-start | bytes 19972
  216.6 4.1 %copy-start.3 = (f32[8,1664]{1,0:T(8,128)S(1)}, f32[8,1664]{1,0:T(8,128)}, u32[]{:S(2)}) copy-start(f32[8,1664]{1,0:T(8,128)} %param.34) | copy-start | bytes 159748
  216.6 4.1 %copy-start.4 = (f32[8,1664]{1,0:T(8,128)S(1)}, f32[8,1664]{1,0:T(8,128)}, u32[]{:S(2)}) copy-start(f32[8,1664]{1,0:T(8,128)} %param.35) | copy-start | bytes 159748
  216.6 29.0 %copy-start.5 = (f32[8,1280]{1,0:T(8,128)S(1)}, f32[8,1280]{1,0:T(8,128)}, u32[]{:S(2)}) copy-start(f32[8,1280]{1,0:T(8,128)} %param.26) | copy-start | bytes 122884
  216.6 28.9 %all-to-all-start = ((f32[8,8,3,1280]{3,1,2,0:T(8,128)}), f32[8,8,3,1280]{3,1,2,0:T(8,128)S(1)}, u32[]{:S(2)}, u32[]{:S(2)}) async-start(f32[8,8,3,1280]{3,1,2,0:T(8,128)} %copy.60), calls=%async_computation | async-start | bytes 1966080 | tf_op jit(solution)/shard_map/all_to_all | solution.py:40
  220.7 25.7 %copy-start.1 = (f32[8,2,1280]{2,1,0:T(2,128)S(1)}, f32[8,2,1280]{2,1,0:T(2,128)}, u32[]{:S(2)}) copy-start(f32[8,2,1280]{2,1,0:T(2,128)} %param.25) | copy-start | bytes 245764
Sparse Core Ops, SparseCore 0:
  9.9 38.6 all-gather.2
where the time goes:
time: 283 us; the launch traced here: 281 us
  matrix products  94.7 us (33%)
  blocking collectives  92.8 us (33%)
  local copies, waits for them, and re-layouts  24.9 us (9%)
  waiting for transfers between devices  24.1 us (9%)
  loops' own time  20.3 us (7%)
  between operations  14.4 us (5%)
  other arithmetic  5.73 us (2%)
  starting transfers between devices  4.05 us (1%)
    all_gather x1, blocking collectives, turned_gather(): whole = lax.all_gather(both, axis, axis=0, tiled=True)  67.2 us
    dot_general x20, matrix products, add_block(): jnp.dot(segment, onehot, precision=lax.Precision.HIGHEST, preferred_eleme...  47.9 us
    dot_general x10, matrix products, one_block(): jnp.dot(values, onehot, precision=lax.Precision.HIGHEST, preferred_elemen...  46.8 us
    all_to_all x2, blocking collectives, sent_to_all(): return lax.all_to_all(copies, axis, split_axis=0, concat_axis=0, tiled=True)  25.6 us
    all_to_all x1, waiting for transfers between devices, summed_on_arrival(): lax.all_to_all(in_blocks(array, dim, peers), axis, 0, 0, tiled=True)  24 us
    dynamic_slice x30, local copies, waits for them, and re-layouts, select_cols(): result, _ = lax.scan(add_block, start_zero, (tiles, numbers))  17.6 us
    another operation x2, loops' own time, select_cols(): result, _ = lax.scan(add_block, start_zero, (tiles, numbers))  13.7 us
    another operation x1, loops' own time, spread_rows(): _, pieces = lax.scan(one_block, jnp.int32(0), numbers)  6.61 us
  transfers between devices with their start and end apart: 2, of which 1 were waited for; matrix products, arithmetic and copies ran while one was open for 1% of the time, Pallas kernels for 0%

commit v1 on v0

v1 whole, which is shorter than its diff:
```python
import jax
import jax.numpy as jnp
from jax import lax
from jax.experimental import pallas as pl
from jax.experimental.pallas import tpu as pltpu
from jax.sharding import PartitionSpec as P

F32 = jnp.float32
BF16 = jnp.bfloat16

DVM, DVA, MP, MQ, INJ, ANG, LIVE, ROOM, COMP, CONST, VM, VA = 0, 10, 20, 30, 40, 60, 70, 83, 96, 97, 100, 103
ROWS1 = 112
ROWS2 = 32
LIM3, SQ3 = 30, 43
ROWS3 = 48
HI = 40
HIP = 48


def pack_kernel(where, vm, va, ds, mu, inj, ang, fb, tb, g, b, h, rt, st, sl, zd, out, table, line):
    for q in range(2):
        for t in range(10):
            lanes = slice(t * 128, t * 128 + 128)
            out[:, DVM + q * 10 + t, :] = ds[:, q, lanes]
            out[:, MP + q * 10 + t, :] = mu[:, q, lanes]
            out[:, INJ + q * 10 + t, :] = inj[:, q, lanes]
    for t in range(10):
        out[:, ANG + t, :] = ang[:, t * 128 : t * 128 + 128]
    comp = jnp.zeros((8, 128), F32)
    for t in range(13):
        lanes = slice(t * 128, t * 128 + 128)
        live = st[:, lanes].astype(F32)
        slack = sl[:, lanes]
        limit = rt[t : t + 1, :]
        out[:, LIVE + t, :] = live
        out[:, ROOM + t, :] = slack - limit * limit
        gap = live * (zd[:, lanes] * slack - 0.01)
        comp = comp + gap * gap
    out[:, COMP, :] = comp
    table[0:13, :] = fb[...].astype(F32)
    table[13:26, :] = tb[...].astype(F32)
    table[26:39, :] = g[...]
    table[39:52, :] = b[...]
    table[52:65, :] = h[...]
    table[65:96, :] = jnp.zeros((31, 128), F32)
    for k in range(3):
        row = table[pl.ds(where[0] + 32 * k, 1), :]
        out[:, CONST + k, :] = jnp.broadcast_to(row, (8, 128))
    lane = lax.broadcasted_iota(jnp.int32, (8, 128), 1)
    shift = where[1]
    first = where[2]
    for ref, at in ((vm, VM), (va, VA)):
        line[...] = jnp.zeros((8, 128), F32)
        line[:, 0:40] = jnp.broadcast_to(ref[...], (8, 40))
        turned = pltpu.roll(line[...], shift, 1)
        for r in range(3):
            in_first = jnp.logical_and(first == r, lane >= shift)
            in_next = jnp.logical_and(first + 1 == r, lane < shift)
            out[:, at + r, :] = jnp.where(jnp.logical_or(in_first, in_next), turned, 0.0)
    for r in range(106, ROWS1):
        out[:, r, :] = jnp.zeros((8, 128), F32)


def spread_kernel(part, out, line):
    for k in range(3):
        line[8 * k : 8 * k + 8, :] = part[:, CONST - 96 + k, :]
    both = part[0, VM - 96 : VM - 96 + 6, :]
    for b in range(1, 8):
        both = both + part[b, VM - 96 : VM - 96 + 6, :]
    line[24:30, :] = both
    line[30:32, :] = jnp.zeros((2, 128), F32)
    whole = line[...]
    for c in range(32):
        out[c] = whole


def in_two(x):
    high = x.astype(BF16)
    low = (x - high.astype(F32)).astype(BF16)
    return high, low


def main_kernel(r1, r2, out, tab, split, onehot, got, lows, highs, vals, left, acc, numbers, sums):
    for n in range(80):
        b, t = divmod(n, 10)
        m, s = divmod(n, 5)
        for q, (at, row) in enumerate(((DVM, 24), (DVA, 27))):
            if s < 2:
                base = r2[2 * m, row + s : row + s + 1, :]
            elif s == 2:
                base = r2[2 * m, row + 2 : row + 3, :] + r2[2 * m + 1, row : row + 1, :]
            else:
                base = r2[2 * m + 1, row + s - 2 : row + s - 1, :]
            lanes = slice((n % 2) * 128, (n % 2) * 128 + 128)
            tab[q * HI + n // 2 : q * HI + n // 2 + 1, lanes] = base + r1[b, at + t : at + t + 1, :]
        for q, at in ((2, MP), (3, MQ)):
            lanes = slice((n % 2) * 128, (n % 2) * 128 + 128)
            tab[q * HI + n // 2 : q * HI + n // 2 + 1, lanes] = r1[b, at + t : at + t + 1, :]
    high, low = in_two(tab[...])
    split[:, 0:256] = high
    split[:, 256:512] = low
    acc[...] = jnp.zeros((6 * HIP, 256), F32)
    numbers[...] = lax.broadcasted_iota(jnp.int32, (256, 128), 0).astype(F32).astype(BF16)
    rows_hi = lax.broadcasted_iota(jnp.int32, (HI, 128), 0).astype(F32)

    def constant(p, t):
        k, c = divmod(p * 13 + t, 32)
        return r2[c, 8 * k : 8 * k + 8, :]

    lim_sq = jnp.zeros((8, 128), F32)
    for t in range(13):
        for e in range(2):
            index = constant(e, t)
            hi = jnp.floor(index * (1.0 / 256.0))
            highs[e] = hi
            lows[e] = index - hi * 256.0
            for r in range(8):
                row = jnp.broadcast_to(lows[e, r : r + 1, :], (256, 128)).astype(BF16)
                onehot[e, :, r * 128 : r * 128 + 128] = jnp.where(numbers[...] == row, 1.0, 0.0).astype(BF16)
            weights = onehot[e]
            picked = jnp.dot(split[...], jnp.concatenate([weights, weights], 0), preferred_element_type=F32)
            for r in range(8):
                mask = jnp.broadcast_to(highs[e, r : r + 1, :], (HI, 128)) == rows_hi
                for q in range(4):
                    part = picked[q * HI : q * HI + HI, r * 128 : r * 128 + 128]
                    got[e * 4 + q, r : r + 1, :] = jnp.sum(jnp.where(mask, part, 0.0), axis=0, keepdims=True)
        g, b, h = constant(2, t), constant(3, t), constant(4, t)
        live = r1[:, LIVE + t, :]
        room = r1[:, ROOM + t, :]
        vf, vt = got[0], got[4]
        turn = got[1] - got[5]
        cs, sn = jnp.cos(turn), jnp.sin(turn)
        u = vf * vt
        gc, bs, gs, bc = g * cs, b * sn, g * sn, b * cs
        pf = live * (g * vf * vf - u * (gc + bs))
        qf = live * (-(b + h) * vf * vf - u * (gs - bc))
        pt = live * (g * vt * vt - u * (gc - bs))
        qt = live * (-(b + h) * vt * vt + u * (gs + bc))
        fd = live * u * (got[2] * (gs - bc) - got[3] * (gc + bs) + got[6] * (gs + bc) + got[7] * (gc - bs))
        limit = live * (pf * pf + qf * qf + room)
        out[:, LIM3 + t, :] = limit
        lim_sq = lim_sq + limit * limit
        for e, three in enumerate(((pf, qf, fd), (pt, qt, -fd))):
            for k in range(3):
                vals[e * 3 + k] = three[k]
        for e in range(2):
            for r in range(8):
                mask = numbers[0:HIP, :] == jnp.broadcast_to(highs[e, r : r + 1, :], (HIP, 128)).astype(BF16)
                lanes = slice(r * 128, r * 128 + 128)
                for k in range(3):
                    high, low = in_two(jnp.broadcast_to(vals[e * 3 + k, r : r + 1, :], (HIP, 128)))
                    zero = jnp.zeros((HIP, 128), BF16)
                    left[e, k * HIP : k * HIP + HIP, lanes] = jnp.where(mask, high, zero)
                    left[e, (k + 3) * HIP : (k + 4) * HIP, lanes] = jnp.where(mask, low, zero)
            acc[...] += lax.dot_general(left[e], onehot[e], (((1,), (1,)), ((), ())), preferred_element_type=F32)

    mis_sq = jnp.zeros((8, 128), F32)
    dual_sq = jnp.zeros((8, 128), F32)
    for k in range(3):
        for half in range(2):
            sums[half, k * HIP : k * HIP + HIP, :] = (
                acc[k * HIP : k * HIP + HIP, half * 128 : half * 128 + 128]
                + acc[(k + 3) * HIP : (k + 4) * HIP, half * 128 : half * 128 + 128]
            )
    for k in range(3):
        for t in range(10):
            total = sums[t % 2, pl.ds(k * HIP + t // 2, 8, stride=5), :]
            if k < 2:
                total = total - r1[:, INJ + k * 10 + t, :]
                mis_sq = mis_sq + total * total
            else:
                total = total + r1[:, ANG + t, :]
                dual_sq = dual_sq + total * total
            out[:, k * 10 + t, :] = total
    lane = lax.broadcasted_iota(jnp.int32, (8, 128), 1)
    squares = jnp.zeros((8, 128), F32)
    for k, part in enumerate((mis_sq, dual_sq, lim_sq, r1[:, COMP, :])):
        squares = jnp.where(lane == k, jnp.sum(part), squares)
    out[:, SQ3, :] = squares
    for r in range(SQ3 + 1, ROWS3):
        out[:, r, :] = jnp.zeros((8, 128), F32)


def norms_kernel(part, norms, out):
    squares = part[:, SQ3 - 40, :]
    norms[...] = jnp.sqrt(squares)[:, 0:4]
    total = jnp.sum(squares, axis=0, keepdims=True)
    out[...] = jnp.broadcast_to(total[None], (32, 1, 128))


def unpack_kernel(r3, mismatch, dual, limit):
    for t in range(10):
        lanes = slice(t * 128, t * 128 + 128)
        for k in range(2):
            mismatch[:, k, lanes] = r3[:, k * 10 + t, :]
        dual[:, lanes] = r3[:, 20 + t, :]
    for t in range(13):
        limit[:, t * 128 : t * 128 + 128] = r3[:, LIM3 + t, :]


def total_kernel(r4, out):
    total = jnp.sum(r4[:, 0, :], axis=0, keepdims=True)
    out[...] = jnp.sqrt(total * (1.0 / 256.0))


def of(shape, dtype=F32):
    return jax.ShapeDtypeStruct(shape, dtype)


def per_device(vm, va, ds, mu, inj, ang, fb, tb, st, g, b, h, rt, sl, zd):
    c, me = lax.axis_index("ctg"), lax.axis_index("br")
    offset = (c % 2) * 64 + me * 40
    where = jnp.stack([c, offset % 128, offset // 128]).astype(jnp.int32)
    sixth = [x.reshape(13, 128) for x in (fb, tb, g, b, h, rt)]
    vmem = pl.BlockSpec(memory_space=pltpu.VMEM)
    send1 = pl.pallas_call(
        pack_kernel,
        out_shape=of((8, ROWS1, 128)),
        in_specs=[pl.BlockSpec(memory_space=pltpu.SMEM)] + [vmem] * 15,
        scratch_shapes=[pltpu.VMEM((96, 128), F32), pltpu.VMEM((8, 128), F32)],
        name="pack",
    )(where, vm.reshape(1, 40), va.reshape(1, 40), ds, mu, inj, ang, *sixth, st, sl, zd)
    r1 = lax.all_to_all(send1, "br", 0, 0, tiled=True)
    send2 = pl.pallas_call(
        spread_kernel,
        grid=(1,),
        in_specs=[pl.BlockSpec((8, 16, 128), lambda i: (0, 6, 0))],
        out_specs=pl.BlockSpec((32, ROWS2, 128), lambda i: (0, 0, 0)),
        out_shape=of((32, ROWS2, 128)),
        scratch_shapes=[pltpu.VMEM((ROWS2, 128), F32)],
        name="spread",
    )(r1)
    r2 = lax.all_to_all(send2, "ctg", 0, 0, tiled=True)
    send3 = pl.pallas_call(
        main_kernel,
        out_shape=of((8, ROWS3, 128)),
        scratch_shapes=[
            pltpu.VMEM((4 * HI, 256), F32),
            pltpu.VMEM((4 * HI, 512), BF16),
            pltpu.VMEM((2, 256, 1024), BF16),
            pltpu.VMEM((8, 8, 128), F32),
            pltpu.VMEM((2, 8, 128), F32),
            pltpu.VMEM((2, 8, 128), F32),
            pltpu.VMEM((6, 8, 128), F32),
            pltpu.VMEM((2, 6 * HIP, 1024), BF16),
            pltpu.VMEM((6 * HIP, 256), F32),
            pltpu.VMEM((256, 128), BF16),
            pltpu.VMEM((2, 3 * HIP, 128), F32),
        ],
        name="main",
    )(r1, r2)
    r3 = lax.all_to_all(send3, "br", 0, 0, tiled=True)
    norms, send4 = pl.pallas_call(
        norms_kernel,
        grid=(1,),
        in_specs=[pl.BlockSpec((8, 8, 128), lambda i: (0, 5, 0))],
        out_specs=(pl.BlockSpec((8, 4), lambda i: (0, 0)), pl.BlockSpec((32, 1, 128), lambda i: (0, 0, 0))),
        out_shape=(of((8, 4)), of((32, 1, 128))),
        name="norms",
    )(r3)
    r4 = lax.all_to_all(send4, "ctg", 0, 0, tiled=True)
    mismatch, dual, limit = pl.pallas_call(
        unpack_kernel, out_shape=(of((8, 2, 1280)), of((8, 1280)), of((8, 1664))), name="unpack"
    )(r3)
    total = pl.pallas_call(total_kernel, out_shape=of((1, 128)), name="total")(r4)
    return mismatch, dual, limit, norms, total[0, 0:4]


def solution(mesh):
    both, scen, line = P(("ctg", "br")), P("ctg", "br"), P("br")
    bus = P("ctg", None, "br")
    placed = (both, both, bus, bus, bus, scen, line, line, scen, line, line, line, line, scen, scen)
    return jax.shard_map(
        per_device,
        mesh=mesh,
        in_specs=placed,
        out_specs=(bus, scen, scen, P("ctg", None), P()),
        check_vma=False,
    )
```

time: 283 us -> 99.4 us (0.35)
  matrix products: 94.7 us -> 0 us
  blocking collectives: 92.8 us -> 59.9 us
  Pallas kernels: 0 us -> 26.4 us
  local copies, waits for them, and re-layouts: 24.9 us -> 2.44 us
  loops' own time: 20.3 us -> 0 us
  waiting for transfers between devices: 24.1 us -> 4.71 us
  between operations: 14.4 us -> 0.69 us
  other arithmetic: 5.73 us -> 0.59 us
    dot_general x30 -> x0, matrix products: 94.7 us -> none  [the longest x20 47.9 us: add_block(): jnp.dot(segment, onehot, precision=lax.Precision.HIGHEST, preferred_eleme...]
    all_gather x1 -> x0, blocking collectives: 67.2 us -> none  [turned_gather(): whole = lax.all_gather(both, axis, axis=0, tiled=True)]
    all_to_all x2 -> x3, blocking collectives: 25.6 us -> 59.9 us  [the longest x1 23.9 us: per_device(): r1 = lax.all_to_all(send1, 'br', 0, 0, tiled=True)]
    pallas_call x0 -> x6, Pallas kernels: none -> 26.4 us  [the longest x1 18.1 us: per_device(): pl.pallas_call(main_kernel, out_shape=of((8, ROWS3, 128)), scratch_shapes...]
    another operation x3 -> x0, loops' own time: 20.3 us -> none  [the longest x2 13.7 us: select_cols(): result, _ = lax.scan(add_block, start_zero, (tiles, numbers))]
    all_to_all x1, waiting for transfers between devices: 24 us -> 4.71 us  [per_device(): r4 = lax.all_to_all(send4, 'ctg', 0, 0, tiled=True)]
    dynamic_slice x30 -> x0, local copies, waits for them, and re-layouts: 17.6 us -> none  [select_cols(): result, _ = lax.scan(add_block, start_zero, (tiles, numbers))]
    reduce_sum x7 -> x0, other arithmetic: 3.07 us -> none  [the longest x1 0.8 us: per_device(): limit_part = jnp.sum(limit_res * limit_res, axis=1)]
  transfers between devices with their start and end apart: 2 -> 1, of which waited for: 1 -> 1; matrix products, arithmetic and copies ran while one was open for 1% -> 1% of each run, Pallas kernels for 0% -> 2%
where the time goes in v1:
time: 99.4 us; the launch traced here: 98.7 us
  blocking collectives  59.9 us (60%)
  Pallas kernels  26.4 us (27%)
  waiting for transfers between devices  4.71 us (5%)
  starting transfers between devices  3.94 us (4%)
  local copies, waits for them, and re-layouts  2.44 us (2%)
    all_to_all x1, blocking collectives, per_device(): r1 = lax.all_to_all(send1, 'br', 0, 0, tiled=True)  23.9 us
    all_to_all x1, blocking collectives, per_device(): r2 = lax.all_to_all(send2, 'ctg', 0, 0, tiled=True)  21 us
    pallas_call x1, Pallas kernels, per_device(): pl.pallas_call(main_kernel, out_shape=of((8, ROWS3, 128)), scratch_shapes...  18.1 us
    all_to_all x1, blocking collectives, per_device(): r3 = lax.all_to_all(send3, 'br', 0, 0, tiled=True)  15 us
    all_to_all x1, waiting for transfers between devices, per_device(): r4 = lax.all_to_all(send4, 'ctg', 0, 0, tiled=True)  4.71 us
    all_to_all x1, starting transfers between devices, per_device(): r4 = lax.all_to_all(send4, 'ctg', 0, 0, tiled=True)  3.94 us
    pallas_call x1, Pallas kernels, per_device(): pl.pallas_call(pack_kernel, out_shape=of((8, ROWS1, 128)), in_specs=[pl.B...  2.18 us
  transfers between devices with their start and end apart: 1, of which 1 were waited for; matrix products, arithmetic and copies ran while one was open for 1% of the time, Pallas kernels for 2%

profile of v1, /device:TPU:1, one launch (start us, length us, event | category | flops | bytes accessed | tf_op | source)
XLA Modules:
  0.0 98.7 jit_solution(17280234932792243336)
XLA Ops:
  0.7 0.6 pad_add_fusion.where
  1.3 2.2 %pack.1 = f32[8,112,128]{2,1,0:T(8,128)} custom-call(s32[3]{0:T(128)} %pad_add_fusion.where, f32[1,40]{1,0:T(1,128)} %bitcast.19, f32[1,40]{1,0:T(1,128)} %bitcast.20, f32[8,2,1280]{2,1,0:T(2,128)} %ds.1, f32[8,2,1280]{2,1,0:T(2,128)} %mu.1, f32[8,2,1280]{2,1,0:T(2,128)} %inj.1, f32[8,1280]{1,0:T(8,128)} %ang.1, s32[13,128]{1,0:T(8,128)} %bitcast.13, ...), custom_call_target="tpu_custom_call" | custom-call | tf_op jit(solution)/shard_map/pack/pallas_call | solution.py:216
  3.4 23.9 %all_to_all.20.part.r1 = f32[8,112,128]{2,1,0:T(8,128)} all-to-all(f32[8,112,128]{2,1,0:T(8,128)} %pack.1), channel_id=1, replica_groups=mesh['ctg'=32,'br'=8] {'br'}, dimensions={0} | all-to-all | bytes 917504 | tf_op jit(solution)/shard_map/all_to_all | solution.py:223
  27.4 1.7 %spread.1 = f32[32,32,128]{2,1,0:T(8,128)} custom-call(f32[8,112,128]{2,1,0:T(8,128)} %all_to_all.20.part.r1), custom_call_target="tpu_custom_call" | custom-call | tf_op jit(solution)/shard_map/spread/pallas_call | solution.py:224
  29.1 21.0 %all_to_all.21.r2 = f32[32,32,128]{2,1,0:T(8,128)} all-to-all(f32[32,32,128]{2,1,0:T(8,128)} %spread.1), channel_id=1, replica_groups=mesh['ctg'=32,'br'=8] {'ctg'}, dimensions={0} | all-to-all | bytes 1048576 | tf_op jit(solution)/shard_map/all_to_all | solution.py:233
  50.1 18.1 %main.1 = f32[8,48,128]{2,1,0:T(8,128)} custom-call(f32[8,112,128]{2,1,0:T(8,128)} %all_to_all.20.part.r1, f32[32,32,128]{2,1,0:T(8,128)} %all_to_all.21.r2), custom_call_target="tpu_custom_call" | custom-call | tf_op jit(solution)/shard_map/main/pallas_call | solution.py:234
  68.2 15.0 %all_to_all.22.r3.part = f32[8,48,128]{2,1,0:T(8,128)} all-to-all(f32[8,48,128]{2,1,0:T(8,128)} %main.1), channel_id=1, replica_groups=mesh['ctg'=32,'br'=8] {'br'}, dimensions={0} | all-to-all | bytes 393216 | tf_op jit(solution)/shard_map/all_to_all | solution.py:252
  83.2 1.4 %norms.1 = (f32[8,4]{1,0:T(8,128)}, f32[32,1,128]{2,1,0:T(1,128)}) custom-call(f32[8,48,128]{2,1,0:T(8,128)} %all_to_all.22.r3.part), custom_call_target="tpu_custom_call" | custom-call | tf_op jit(solution)/shard_map/norms/pallas_call | solution.py:253
  84.6 0.0 copy-start.1
  84.6 3.9 %all-to-all-start.3 = ((f32[32,1,128]{2,1,0:T(1,128)}), f32[32,1,128]{2,1,0:T(1,128)S(1)}, u32[]{:S(2)}, u32[]{:S(2)}) async-start(f32[32,1,128]{2,1,0:T(1,128)} %get-tuple-element.14), calls=%async_computation.3 | async-start | bytes 32768 | tf_op jit(solution)/shard_map/all_to_all | solution.py:261
  88.5 0.0 copy-done.1
  88.5 0.7 copy.20
  89.2 1.7 %unpack.1 = (f32[8,2,1280]{2,1,0:T(2,128)}, f32[8,1280]{1,0:T(8,128)}, f32[8,1664]{1,0:T(8,128)}) custom-call(f32[8,48,128]{2,1,0:T(8,128)} %all_to_all.22.r3.part), custom_call_target="tpu_custom_call" | custom-call | tf_op jit(solution)/shard_map/unpack/pallas_call | solution.py:262
  90.9 4.7 %all-to-all-done.3.r4 = f32[32,1,128]{2,1,0:T(1,128)S(1)} async-done(((f32[32,1,128]{2,1,0:T(1,128)}), f32[32,1,128]{2,1,0:T(1,128)S(1)}, u32[]{:S(2)}, u32[]{:S(2)}) %all-to-all-start.3) | async-done | bytes 16416 | tf_op jit(solution)/shard_map/all_to_all | solution.py:261
  95.6 0.0 copy-start
  95.6 0.6 copy-done
  96.2 1.3 %total.1 = f32[1,128]{1,0:T(1,128)} custom-call(f32[32,1,128]{2,1,0:T(1,128)} %copy-done), custom_call_target="tpu_custom_call" | custom-call | tf_op jit(solution)/shard_map/total/pallas_call | solution.py:265
  97.5 1.2 %slice_bitcast_fusion = f32[4]{0:T(128)} fusion(f32[1,128]{1,0:T(1,128)} %total.1), kind=kLoop, calls=%fused_computation.1 | loop fusion | bytes 32 | tf_op jit(solution)/shard_map/squeeze | solution.py:266
Async XLA Ops:
  84.6 3.9 %copy-start.1 = (f32[8,4]{1,0:T(8,128)S(1)}, f32[8,4]{1,0:T(8,128)}, u32[]{:S(2)}) copy-start(f32[8,4]{1,0:T(8,128)} %get-tuple-element.18) | copy-start | bytes 388
  84.6 11.0 %all-to-all-start.3 = ((f32[32,1,128]{2,1,0:T(1,128)}), f32[32,1,128]{2,1,0:T(1,128)S(1)}, u32[]{:S(2)}, u32[]{:S(2)}) async-start(f32[32,1,128]{2,1,0:T(1,128)} %get-tuple-element.14), calls=%async_computation.3 | async-start | bytes 32768 | tf_op jit(solution)/shard_map/all_to_all | solution.py:261
  95.6 0.6 copy-start

commit v2 on v1

v2 whole, which is shorter than its diff:
```python
import jax
import jax.numpy as jnp
from jax import lax
from jax.experimental import pallas as pl
from jax.experimental.pallas import tpu as pltpu
from jax.sharding import PartitionSpec as P

F32 = jnp.float32
BF16 = jnp.bfloat16

DVM, DVA, MP, MQ, INJ, ANG, LIVE, ROOM, COMP, BASE, LAST, CONST = 0, 10, 20, 30, 40, 60, 70, 83, 96, 97, 98, 99
ROWS1 = 104
VM2, VA2 = 16, 19
ROWS2 = 24
LIM3, SQ3 = 30, 43
ROWS3 = 48
HI = 40
HIP = 48


def pack_kernel(vm, va, ds, mu, inj, ang, fb, tb, g, b, h, rt, st, sl, zd, out, table, line):
    c, me = lax.axis_index("ctg"), lax.axis_index("br")
    for q in range(2):
        for t in range(10):
            lanes = slice(t * 128, t * 128 + 128)
            out[:, DVM + q * 10 + t, :] = ds[:, q, lanes]
            out[:, MP + q * 10 + t, :] = mu[:, q, lanes]
            out[:, INJ + q * 10 + t, :] = inj[:, q, lanes]
    for t in range(10):
        out[:, ANG + t, :] = ang[:, t * 128 : t * 128 + 128]
    comp = jnp.zeros((8, 128), F32)
    for t in range(13):
        lanes = slice(t * 128, t * 128 + 128)
        live = st[:, lanes].astype(F32)
        slack = sl[:, lanes]
        limit = rt[t : t + 1, :]
        out[:, LIVE + t, :] = live
        out[:, ROOM + t, :] = slack - limit * limit
        gap = live * (zd[:, lanes] * slack - 0.01)
        comp = comp + gap * gap
    out[:, COMP, :] = comp
    table[0:13, :] = fb[...].astype(F32)
    table[13:26, :] = tb[...].astype(F32)
    table[26:39, :] = g[...]
    table[39:52, :] = b[...]
    table[52:65, :] = h[...]
    for k in range(2):
        row = table[pl.ds(c + 32 * k, 1), :]
        out[:, CONST + k, :] = jnp.broadcast_to(row, (8, 128))
    out[:, LAST, :] = jnp.broadcast_to(h[12:13, :], (8, 128))
    shift = lax.rem((c % 2) * 64 + me * 40, 128)
    line[...] = jnp.zeros((8, 128), F32)
    line[:, 0:40] = jnp.broadcast_to(vm[...], (8, 40))
    turned = pltpu.roll(line[...], shift, 1)
    line[:, 0:40] = jnp.broadcast_to(va[...], (8, 40))
    out[:, BASE, :] = turned + pltpu.roll(line[...], lax.rem(shift + 64, 128), 1)
    for r in range(CONST + 2, ROWS1):
        out[:, r, :] = jnp.zeros((8, 128), F32)


def spread_kernel(part, out, line):
    for k in range(2):
        line[8 * k : 8 * k + 8, :] = part[:, CONST - 96 + k, :]
    c = lax.axis_index("ctg")
    start = lax.broadcasted_iota(jnp.int32, (8, 128), 0) * 40 + (c % 2) * 64
    lane = lax.broadcasted_iota(jnp.int32, (8, 128), 1)
    mags = part[:, BASE - 96, :]
    angs = pltpu.roll(mags, 64, 1)
    for r in range(3):
        inside = jnp.logical_and(lane + 128 * r >= start, lane + 128 * r < start + 40)
        line[VM2 + r : VM2 + r + 1, :] = jnp.sum(jnp.where(inside, mags, 0.0), axis=0, keepdims=True)
        line[VA2 + r : VA2 + r + 1, :] = jnp.sum(jnp.where(inside, angs, 0.0), axis=0, keepdims=True)
    line[22:24, :] = jnp.zeros((2, 128), F32)
    whole = line[...]
    for i in range(32):
        out[i] = whole


def in_two(x):
    high = x.astype(BF16)
    low = (x - high.astype(F32)).astype(BF16)
    return high, low


def main_kernel(r1, r2, out, tab, split, consts, sides, acc, sums, *bufs):
    for n in range(80):
        b, t = divmod(n, 10)
        m, s = divmod(n, 5)
        lanes = slice((n % 2) * 128, (n % 2) * 128 + 128)
        for q, (at, row) in enumerate(((DVM, VM2), (DVA, VA2))):
            if s < 2:
                base = r2[2 * m, row + s : row + s + 1, :]
            elif s == 2:
                base = r2[2 * m, row + 2 : row + 3, :] + r2[2 * m + 1, row : row + 1, :]
            else:
                base = r2[2 * m + 1, row + s - 2 : row + s - 1, :]
            tab[q * HI + n // 2 : q * HI + n // 2 + 1, lanes] = base + r1[b, at + t : at + t + 1, :]
        for q, at in ((2, MP), (3, MQ)):
            tab[q * HI + n // 2 : q * HI + n // 2 + 1, lanes] = r1[b, at + t : at + t + 1, :]
    high, low = in_two(tab[...])
    for k in range(2):
        split[k] = high[:, k * 128 : k * 128 + 128]
        split[k + 2] = low[:, k * 128 : k * 128 + 128]
    acc[...] = jnp.zeros((6 * HIP, 256), F32)
    numbers = lax.broadcasted_iota(jnp.int32, (256, 128), 0).astype(F32).astype(BF16)
    for t in range(13):
        for p in range(5):
            k, c = divmod(p * 13 + t, 32)
            consts[p, t] = r2[c, 8 * k : 8 * k + 8, :] if k < 2 else r1[:, LAST, :]
        sides[0, t] = r1[:, LIVE + t, :]
        sides[1, t] = r1[:, ROOM + t, :]
    rows_hi = lax.broadcasted_iota(jnp.int32, (HI, 128), 0).astype(F32)
    one, zero = jnp.ones((256, 128), BF16), jnp.zeros((256, 128), BF16)

    def table():
        return jnp.concatenate([split[k] for k in range(4)], 1)

    def across(ref, r):
        return jnp.broadcast_to(ref[r : r + 1, :], (16, 128))

    def hot(ends, e, r):
        row = across(ends.at[2 * e + 1], r).astype(BF16)
        return jnp.where(numbers == jnp.concatenate([row] * 16, 0), one, zero)

    def gather(t, ends, got, vals):
        for e in range(2):
            index = consts[e, t]
            hi = jnp.floor(index * (1.0 / 256.0))
            ends[2 * e] = hi
            ends[2 * e + 1] = index - hi * 256.0
            for pair in range(4):
                weights = jnp.concatenate([hot(ends, e, 2 * pair), hot(ends, e, 2 * pair + 1)], 1)
                picked = jnp.dot(table(), jnp.concatenate([weights, weights], 0), preferred_element_type=F32)
                for half in range(2):
                    r = 2 * pair + half
                    mask = jnp.broadcast_to(ends[2 * e, r : r + 1, :], (HI, 128)) == rows_hi
                    for q in range(4):
                        part = picked[q * HI : q * HI + HI, half * 128 : half * 128 + 128]
                        got[e * 4 + q, r : r + 1, :] = jnp.sum(jnp.where(mask, part, 0.0), axis=0, keepdims=True)
        g, b, h = consts[2, t], consts[3, t], consts[4, t]
        live, room = sides[0, t], sides[1, t]
        vf, vt = got[0], got[4]
        turn = got[1] - got[5]
        cs, sn = jnp.cos(turn), jnp.sin(turn)
        u = vf * vt
        gc, bs, gs, bc = g * cs, b * sn, g * sn, b * cs
        pf = live * (g * vf * vf - u * (gc + bs))
        qf = live * (-(b + h) * vf * vf - u * (gs - bc))
        pt = live * (g * vt * vt - u * (gc - bs))
        qt = live * (-(b + h) * vt * vt + u * (gs + bc))
        fd = live * u * (got[2] * (gs - bc) - got[3] * (gc + bs) + got[6] * (gs + bc) + got[7] * (gc - bs))
        sides[2, t] = live * (pf * pf + qf * qf + room)
        for k, value in enumerate((pf, qf, fd, pt, qt, -fd)):
            vals[k] = value

    def scatter(ends, got, vals):
        rows, cols = [], []
        for e in range(2):
            for r in range(8):
                row = across(ends.at[2 * e], r).astype(BF16)
                mask = numbers[0:HIP, :] == jnp.concatenate([row] * 3, 0)
                highs, lows = [], []
                for k in range(3):
                    high, low = in_two(across(vals.at[e * 3 + k], r))
                    highs.append(jnp.where(mask, jnp.concatenate([high] * 3, 0), zero[0:HIP]))
                    lows.append(jnp.where(mask, jnp.concatenate([low] * 3, 0), zero[0:HIP]))
                rows.append(jnp.concatenate(highs + lows, 0))
                cols.append(hot(ends, e, r))
        rows, cols = jnp.concatenate(rows, 1), jnp.concatenate(cols, 1)
        acc[...] += lax.dot_general(rows, cols, (((1,), (1,)), ((), ())), preferred_element_type=F32)

    even, odd = bufs[:3], bufs[3:]
    gather(0, *even)

    def two(i, carry):
        gather(2 * i + 1, *odd)
        scatter(*even)
        gather(2 * i + 2, *even)
        scatter(*odd)
        return carry

    lax.fori_loop(0, 6, two, 0)
    scatter(*even)

    lim_sq = jnp.zeros((8, 128), F32)
    for t in range(13):
        limit = sides[2, t]
        out[:, LIM3 + t, :] = limit
        lim_sq = lim_sq + limit * limit
    mis_sq = jnp.zeros((8, 128), F32)
    dual_sq = jnp.zeros((8, 128), F32)
    for k in range(3):
        for half in range(2):
            lanes = slice(half * 128, half * 128 + 128)
            sums[half, k * HIP : k * HIP + HIP, :] = (
                acc[k * HIP : k * HIP + HIP, lanes] + acc[(k + 3) * HIP : (k + 4) * HIP, lanes]
            )
    for k in range(3):
        for t in range(10):
            total = sums[t % 2, pl.ds(k * HIP + t // 2, 8, stride=5), :]
            if k < 2:
                total = total - r1[:, INJ + k * 10 + t, :]
                mis_sq = mis_sq + total * total
            else:
                total = total + r1[:, ANG + t, :]
                dual_sq = dual_sq + total * total
            out[:, k * 10 + t, :] = total
    lane = lax.broadcasted_iota(jnp.int32, (8, 128), 1)
    squares = jnp.zeros((8, 128), F32)
    for k, part in enumerate((mis_sq, dual_sq, lim_sq, r1[:, COMP, :])):
        squares = jnp.where(lane == k, jnp.sum(part), squares)
    out[:, SQ3, :] = squares
    for r in range(SQ3 + 1, ROWS3):
        out[:, r, :] = jnp.zeros((8, 128), F32)


def unpack_kernel(r3, mismatch, dual, limit):
    for t in range(10):
        lanes = slice(t * 128, t * 128 + 128)
        for k in range(2):
            mismatch[:, k, lanes] = r3[:, k * 10 + t, :]
        dual[:, lanes] = r3[:, 20 + t, :]
    for t in range(13):
        limit[:, t * 128 : t * 128 + 128] = r3[:, LIM3 + t, :]


def of(shape, dtype=F32):
    return jax.ShapeDtypeStruct(shape, dtype)


def per_device(vm, va, ds, mu, inj, ang, fb, tb, st, g, b, h, rt, sl, zd):
    sixth = [x.reshape(13, 128) for x in (fb, tb, g, b, h, rt)]
    send1 = pl.pallas_call(
        pack_kernel,
        out_shape=of((8, ROWS1, 128)),
        scratch_shapes=[pltpu.VMEM((96, 128), F32), pltpu.VMEM((8, 128), F32)],
        name="pack",
    )(vm.reshape(1, 40), va.reshape(1, 40), ds, mu, inj, ang, *sixth, st, sl, zd)
    r1 = lax.all_to_all(send1, "br", 0, 0, tiled=True)
    send2 = pl.pallas_call(
        spread_kernel,
        grid=(1,),
        in_specs=[pl.BlockSpec((8, 8, 128), lambda i: (0, 12, 0))],
        out_specs=pl.BlockSpec((32, ROWS2, 128), lambda i: (0, 0, 0)),
        out_shape=of((32, ROWS2, 128)),
        scratch_shapes=[pltpu.VMEM((ROWS2, 128), F32)],
        name="spread",
    )(r1)
    r2 = lax.all_to_all(send2, "ctg", 0, 0, tiled=True)
    send3 = pl.pallas_call(
        main_kernel,
        out_shape=of((8, ROWS3, 128)),
        scratch_shapes=[
            pltpu.VMEM((4 * HI, 256), F32),
            pltpu.VMEM((4, 4 * HI, 128), BF16),
            pltpu.VMEM((5, 13, 8, 128), F32),
            pltpu.VMEM((3, 13, 8, 128), F32),
            pltpu.VMEM((6 * HIP, 256), F32),
            pltpu.VMEM((2, 3 * HIP, 128), F32),
        ]
        + [
            pltpu.VMEM((4, 8, 128), F32),
            pltpu.VMEM((8, 8, 128), F32),
            pltpu.VMEM((6, 8, 128), F32),
        ]
        * 2,
        name="main",
    )(r1, r2)
    r3 = lax.all_to_all(send3, "br", 0, 0, tiled=True)
    squares = r3[:, SQ3, :]
    send4 = jnp.broadcast_to(jnp.sum(squares, axis=0)[None, None], (32, 1, 128))
    r4 = lax.all_to_all(send4, "ctg", 0, 0, tiled=True)
    mismatch, dual, limit = pl.pallas_call(
        unpack_kernel, out_shape=(of((8, 2, 1280)), of((8, 1280)), of((8, 1664))), name="unpack"
    )(r3)
    total = jnp.sqrt(jnp.sum(r4[:, 0, 0:4], axis=0) / 256.0)
    return mismatch, dual, limit, jnp.sqrt(squares[:, 0:4]), total


def solution(mesh):
    both, scen, line = P(("ctg", "br")), P("ctg", "br"), P("br")
    bus = P("ctg", None, "br")
    placed = (both, both, bus, bus, bus, scen, line, line, scen, line, line, line, line, scen, scen)
    return jax.shard_map(
        per_device,
        mesh=mesh,
        in_specs=placed,
        out_specs=(bus, scen, scen, P("ctg", None), P()),
        check_vma=False,
    )
```

time: 99.4 us -> 87.2 us (0.88)
  Pallas kernels: 26.4 us -> 18.3 us
  blocking collectives: 59.9 us -> 57.2 us
  local copies, waits for them, and re-layouts: 2.44 us -> 1.31 us
    pallas_call x1, Pallas kernels: 18.1 us -> 12.8 us  [per_device(): pl.pallas_call(main_kernel, out_shape=of((8, ROWS3, 128)), scratch_shapes...]
    pallas_call x4 -> x2, Pallas kernels: 6.61 us -> 3.75 us  [the longest x1 2.15 us: per_device(): pl.pallas_call(pack_kernel, out_shape=of((8, ROWS1, 128)), scratch_shapes...]
    squeeze x1 -> x0, local copies, waits for them, and re-layouts: 1.19 us -> none  [per_device(): return (mismatch, dual, limit, norms, total[0, 0:4])]
    all_to_all x1, blocking collectives: 21 us -> 19.9 us  [per_device(): r2 = lax.all_to_all(send2, 'ctg', 0, 0, tiled=True)]
where the time goes in v2:
time: 87.2 us; the launch traced here: 86.7 us
  blocking collectives  57.2 us (66%)
  Pallas kernels  18.3 us (21%)
  waiting for transfers between devices  4.72 us (5%)
  starting transfers between devices  3.93 us (5%)
  local copies, waits for them, and re-layouts  1.31 us (2%)
    all_to_all x1, blocking collectives, per_device(): r1 = lax.all_to_all(send1, 'br', 0, 0, tiled=True)  23 us
    all_to_all x1, blocking collectives, per_device(): r2 = lax.all_to_all(send2, 'ctg', 0, 0, tiled=True)  19.9 us
    all_to_all x1, blocking collectives, per_device(): r3 = lax.all_to_all(send3, 'br', 0, 0, tiled=True)  14.3 us
    pallas_call x1, Pallas kernels, per_device(): pl.pallas_call(main_kernel, out_shape=of((8, ROWS3, 128)), scratch_shapes...  12.8 us
    all_to_all x1, waiting for transfers between devices, per_device(): r4 = lax.all_to_all(send4, 'ctg', 0, 0, tiled=True)  4.72 us
    all_to_all x1, starting transfers between devices, per_device(): r4 = lax.all_to_all(send4, 'ctg', 0, 0, tiled=True)  3.93 us
    pallas_call x1, Pallas kernels, per_device(): pl.pallas_call(pack_kernel, out_shape=of((8, ROWS1, 128)), scratch_shapes...  2.15 us
  transfers between devices with their start and end apart: 1, of which 1 were waited for; matrix products, arithmetic and copies ran while one was open for 1% of the time, Pallas kernels for 2%

profile of v2, /device:TPU:1, one launch (start us, length us, event | category | flops | bytes accessed | tf_op | source)
XLA Modules:
  0.0 86.7 jit_solution(7015918476429719228)
XLA Ops:
  0.6 2.2 %pack.1 = f32[8,104,128]{2,1,0:T(8,128)} custom-call(f32[1,40]{1,0:T(1,128)} %bitcast.16, f32[1,40]{1,0:T(1,128)} %bitcast.17, f32[8,2,1280]{2,1,0:T(2,128)} %ds.1, f32[8,2,1280]{2,1,0:T(2,128)} %mu.1, f32[8,2,1280]{2,1,0:T(2,128)} %inj.1, f32[8,1280]{1,0:T(8,128)} %ang.1, s32[13,128]{1,0:T(8,128)} %bitcast.10, s32[13,128]{1,0:T(8,128)} %bitcast.11, ...), custom_call_target="tpu_custom_call" | custom-call | tf_op jit(solution)/shard_map/pack/pallas_call | solution.py:233
  2.8 23.0 %all_to_all.20.part.r1 = f32[8,104,128]{2,1,0:T(8,128)} all-to-all(f32[8,104,128]{2,1,0:T(8,128)} %pack.1), channel_id=1, replica_groups=mesh['ctg'=32,'br'=8] {'br'}, dimensions={0} | all-to-all | bytes 851968 | tf_op jit(solution)/shard_map/all_to_all | solution.py:239
  25.8 1.6 %spread.1 = f32[32,24,128]{2,1,0:T(8,128)} custom-call(f32[8,104,128]{2,1,0:T(8,128)} %all_to_all.20.part.r1), custom_call_target="tpu_custom_call" | custom-call | tf_op jit(solution)/shard_map/spread/pallas_call | solution.py:240
  27.4 19.9 %all_to_all.21.r2 = f32[32,24,128]{2,1,0:T(8,128)} all-to-all(f32[32,24,128]{2,1,0:T(8,128)} %spread.1), channel_id=1, replica_groups=mesh['ctg'=32,'br'=8] {'ctg'}, dimensions={0} | all-to-all | bytes 786432 | tf_op jit(solution)/shard_map/all_to_all | solution.py:249
  47.3 12.8 %main.1 = f32[8,48,128]{2,1,0:T(8,128)} custom-call(f32[8,104,128]{2,1,0:T(8,128)} %all_to_all.20.part.r1, f32[32,24,128]{2,1,0:T(8,128)} %all_to_all.21.r2), custom_call_target="tpu_custom_call" | custom-call | tf_op jit(solution)/shard_map/main/pallas_call | solution.py:250
  60.1 14.3 %all_to_all.22.r3 = f32[8,48,128]{2,1,0:T(8,128)S(1)} all-to-all(f32[8,48,128]{2,1,0:T(8,128)} %main.1), channel_id=1, replica_groups=mesh['ctg'=32,'br'=8] {'br'}, dimensions={0} | all-to-all | bytes 393216 | tf_op jit(solution)/shard_map/all_to_all | solution.py:269
  74.4 0.0 copy-start
  74.4 0.6 broadcast_in_dim.2
  75.1 3.9 %all-to-all-start.3 = ((f32[32,1,128]{2,1,0:T(1,128)}), f32[32,1,128]{2,1,0:T(1,128)S(1)}, u32[]{:S(2)}, u32[]{:S(2)}) async-start(f32[32,1,128]{2,1,0:T(1,128)} %broadcast_in_dim.2), calls=%async_computation.3 | async-start | bytes 32768 | tf_op jit(solution)/shard_map/all_to_all | solution.py:272
  79.0 0.7 copy.23
  79.7 0.0 copy-done
  79.7 1.7 %unpack.1 = (f32[8,2,1280]{2,1,0:T(2,128)}, f32[8,1280]{1,0:T(8,128)}, f32[8,1664]{1,0:T(8,128)}) custom-call(f32[8,48,128]{2,1,0:T(8,128)} %copy-done), custom_call_target="tpu_custom_call" | custom-call | tf_op jit(solution)/shard_map/unpack/pallas_call | solution.py:273
  81.4 4.7 %all-to-all-done.3 = f32[32,1,128]{2,1,0:T(1,128)S(1)} async-done(((f32[32,1,128]{2,1,0:T(1,128)}), f32[32,1,128]{2,1,0:T(1,128)S(1)}, u32[]{:S(2)}, u32[]{:S(2)}) %all-to-all-start.3) | async-done | bytes 16416 | tf_op jit(solution)/shard_map/all_to_all | solution.py:272
  86.1 0.1 slice_reduce_fusion
  86.1 0.5 multiply_sqrt_fusion
  (2 shorter events, 0.0 us)
Async XLA Ops:
  74.4 5.3 %copy-start = (f32[8,48,128]{2,1,0:T(8,128)}, f32[8,48,128]{2,1,0:T(8,128)S(1)}, u32[]{:S(2)}) copy-start(f32[8,48,128]{2,1,0:T(8,128)S(1)} %all_to_all.22.r3) | copy-start | bytes 589828
  75.1 11.0 %all-to-all-start.3 = ((f32[32,1,128]{2,1,0:T(1,128)}), f32[32,1,128]{2,1,0:T(1,128)S(1)}, u32[]{:S(2)}, u32[]{:S(2)}) async-start(f32[32,1,128]{2,1,0:T(1,128)} %broadcast_in_dim.2), calls=%async_computation.3 | async-start | bytes 32768 | tf_op jit(solution)/shard_map/all_to_all | solution.py:272

commit v3 on v2

--- a/solution.py
+++ b/solution.py
@@ -60,11 +60,11 @@
 
 def spread_kernel(part, out, line):
     for k in range(2):
-        line[8 * k : 8 * k + 8, :] = part[:, CONST - 96 + k, :]
+        line[8 * k : 8 * k + 8, :] = part[:, CONST + k, :]
     c = lax.axis_index("ctg")
     start = lax.broadcasted_iota(jnp.int32, (8, 128), 0) * 40 + (c % 2) * 64
     lane = lax.broadcasted_iota(jnp.int32, (8, 128), 1)
-    mags = part[:, BASE - 96, :]
+    mags = part[:, BASE, :]
     angs = pltpu.roll(mags, 64, 1)
     for r in range(3):
         inside = jnp.logical_and(lane + 128 * r >= start, lane + 128 * r < start + 40)
@@ -224,6 +224,13 @@
         limit[:, t * 128 : t * 128 + 128] = r3[:, LIM3 + t, :]
 
 
+VM_SPEC = pl.BlockSpec(memory_space=pltpu.VMEM)
+
+
+def near(x):
+    return pltpu.with_memory_space_constraint(x, pltpu.VMEM)
+
+
 def of(shape, dtype=F32):
     return jax.ShapeDtypeStruct(shape, dtype)
 
@@ -232,24 +239,26 @@
     sixth = [x.reshape(13, 128) for x in (fb, tb, g, b, h, rt)]
     send1 = pl.pallas_call(
         pack_kernel,
-        out_shape=of((8, ROWS1, 128)),
+        out_shape=pltpu.VMEM((8, ROWS1, 128), F32),
+        out_specs=VM_SPEC,
         scratch_shapes=[pltpu.VMEM((96, 128), F32), pltpu.VMEM((8, 128), F32)],
         name="pack",
     )(vm.reshape(1, 40), va.reshape(1, 40), ds, mu, inj, ang, *sixth, st, sl, zd)
     r1 = lax.all_to_all(send1, "br", 0, 0, tiled=True)
     send2 = pl.pallas_call(
         spread_kernel,
-        grid=(1,),
-        in_specs=[pl.BlockSpec((8, 8, 128), lambda i: (0, 12, 0))],
-        out_specs=pl.BlockSpec((32, ROWS2, 128), lambda i: (0, 0, 0)),
-        out_shape=of((32, ROWS2, 128)),
+        in_specs=[VM_SPEC],
+        out_specs=VM_SPEC,
+        out_shape=pltpu.VMEM((32, ROWS2, 128), F32),
         scratch_shapes=[pltpu.VMEM((ROWS2, 128), F32)],
         name="spread",
-    )(r1)
+    )(near(r1))
     r2 = lax.all_to_all(send2, "ctg", 0, 0, tiled=True)
     send3 = pl.pallas_call(
         main_kernel,
-        out_shape=of((8, ROWS3, 128)),
+        out_shape=pltpu.VMEM((8, ROWS3, 128), F32),
+        out_specs=VM_SPEC,
+        in_specs=[VM_SPEC, VM_SPEC],
         scratch_shapes=[
             pltpu.VMEM((4 * HI, 256), F32),
             pltpu.VMEM((4, 4 * HI, 128), BF16),
@@ -265,14 +274,14 @@
         ]
         * 2,
         name="main",
-    )(r1, r2)
+    )(near(r1), near(r2))
     r3 = lax.all_to_all(send3, "br", 0, 0, tiled=True)
     squares = r3[:, SQ3, :]
     send4 = jnp.broadcast_to(jnp.sum(squares, axis=0)[None, None], (32, 1, 128))
     r4 = lax.all_to_all(send4, "ctg", 0, 0, tiled=True)
     mismatch, dual, limit = pl.pallas_call(
-        unpack_kernel, out_shape=(of((8, 2, 1280)), of((8, 1280)), of((8, 1664))), name="unpack"
-    )(r3)
+        unpack_kernel, out_shape=(of((8, 2, 1280)), of((8, 1280)), of((8, 1664))), name="unpack", in_specs=[VM_SPEC]
+    )(near(r3))
     total = jnp.sqrt(jnp.sum(r4[:, 0, 0:4], axis=0) / 256.0)
     return mismatch, dual, limit, jnp.sqrt(squares[:, 0:4]), total
 

time: 87.2 us -> 81.4 us (0.933)
  Pallas kernels: 18.3 us -> 13.3 us
  blocking collectives: 57.2 us -> 55.7 us
  waiting for transfers between devices: 4.72 us -> 5.65 us
    pallas_call x3, Pallas kernels: 16.6 us -> 12.5 us  [the longest x1 11 us: per_device(): pl.pallas_call(main_kernel, out_shape=pltpu.VMEM((8, ROWS3, 128), F32), o...]
    all_to_all x1, waiting for transfers between devices: 4.72 us -> 5.65 us  [per_device(): r4 = lax.all_to_all(send4, 'ctg', 0, 0, tiled=True)]
    pallas_call x1, Pallas kernels: 1.69 us -> 0.77 us  [per_device(): pl.pallas_call(unpack_kernel, out_shape=(of((8, 2, 1280)), of((8, 1280)),...]
    all_to_all x1, blocking collectives: 14.3 us -> 13.4 us  [per_device(): r3 = lax.all_to_all(send3, 'br', 0, 0, tiled=True)]
  transfers between devices with their start and end apart: 1 -> 1, of which waited for: 1 -> 1; matrix products, arithmetic and copies ran while one was open for 1% -> 1% of each run, Pallas kernels for 2% -> 1%
where the time goes in v3:
time: 81.4 us; the launch traced here: 81.1 us
  blocking collectives  55.7 us (68%)
  Pallas kernels  13.3 us (16%)
  waiting for transfers between devices  5.65 us (7%)
  starting transfers between devices  3.93 us (5%)
  local copies, waits for them, and re-layouts  1.27 us (2%)
    all_to_all x1, blocking collectives, per_device(): r1 = lax.all_to_all(send1, 'br', 0, 0, tiled=True)  22.7 us
    all_to_all x1, blocking collectives, per_device(): r2 = lax.all_to_all(send2, 'ctg', 0, 0, tiled=True)  19.6 us
    all_to_all x1, blocking collectives, per_device(): r3 = lax.all_to_all(send3, 'br', 0, 0, tiled=True)  13.4 us
    pallas_call x1, Pallas kernels, per_device(): pl.pallas_call(main_kernel, out_shape=pltpu.VMEM((8, ROWS3, 128), F32), o...  11 us
    all_to_all x1, waiting for transfers between devices, per_device(): r4 = lax.all_to_all(send4, 'ctg', 0, 0, tiled=True)  5.65 us
    all_to_all x1, starting transfers between devices, per_device(): r4 = lax.all_to_all(send4, 'ctg', 0, 0, tiled=True)  3.93 us
  transfers between devices with their start and end apart: 1, of which 1 were waited for; matrix products, arithmetic and copies ran while one was open for 1% of the time, Pallas kernels for 1%

profile of v3, /device:TPU:1, one launch (start us, length us, event | category | flops | bytes accessed | tf_op | source)
XLA Modules:
  0.0 81.1 jit_solution(8801919343611854105)
XLA Ops:
  0.6 1.4 %pack.1 = f32[8,104,128]{2,1,0:T(8,128)S(1)} custom-call(f32[1,40]{1,0:T(1,128)} %bitcast.16, f32[1,40]{1,0:T(1,128)} %bitcast.17, f32[8,2,1280]{2,1,0:T(2,128)} %ds.1, f32[8,2,1280]{2,1,0:T(2,128)} %mu.1, f32[8,2,1280]{2,1,0:T(2,128)} %inj.1, f32[8,1280]{1,0:T(8,128)} %ang.1, s32[13,128]{1,0:T(8,128)} %bitcast.10, s32[13,128]{1,0:T(8,128)} %bitcast.11, ...), custom_call_target="tpu_custom_call" | custom-call | tf_op jit(solution)/shard_map/pack/pallas_call | solution.py:240
  2.0 22.7 %all_to_all.20.part.r1 = f32[8,104,128]{2,1,0:T(8,128)S(1)} all-to-all(f32[8,104,128]{2,1,0:T(8,128)S(1)} %pack.1), channel_id=1, replica_groups=mesh['ctg'=32,'br'=8] {'br'}, dimensions={0} | all-to-all | bytes 851968 | tf_op jit(solution)/shard_map/all_to_all | solution.py:247
  24.7 0.1 spread.1
  24.8 19.6 %all_to_all.21.r2 = f32[32,24,128]{2,1,0:T(8,128)S(1)} all-to-all(f32[32,24,128]{2,1,0:T(8,128)S(1)} %spread.1), channel_id=1, replica_groups=mesh['ctg'=32,'br'=8] {'ctg'}, dimensions={0} | all-to-all | bytes 786432 | tf_op jit(solution)/shard_map/all_to_all | solution.py:256
  44.4 11.0 %main.1 = f32[8,48,128]{2,1,0:T(8,128)S(1)} custom-call(f32[8,104,128]{2,1,0:T(8,128)S(1)} %all_to_all.20.part.r1, f32[32,24,128]{2,1,0:T(8,128)S(1)} %all_to_all.21.r2), custom_call_target="tpu_custom_call" | custom-call | tf_op jit(solution)/shard_map/main/pallas_call | solution.py:257
  55.5 13.4 %all_to_all.22.r3 = f32[8,48,128]{2,1,0:T(8,128)S(1)} all-to-all(f32[8,48,128]{2,1,0:T(8,128)S(1)} %main.1), channel_id=1, replica_groups=mesh['ctg'=32,'br'=8] {'br'}, dimensions={0} | all-to-all | bytes 393216 | tf_op jit(solution)/shard_map/all_to_all | solution.py:278
  68.9 0.6 broadcast_in_dim.2
  69.5 3.9 %all-to-all-start.3 = ((f32[32,1,128]{2,1,0:T(1,128)}), f32[32,1,128]{2,1,0:T(1,128)S(1)}, u32[]{:S(2)}, u32[]{:S(2)}) async-start(f32[32,1,128]{2,1,0:T(1,128)} %broadcast_in_dim.2), calls=%async_computation.3 | async-start | bytes 32768 | tf_op jit(solution)/shard_map/all_to_all | solution.py:281
  73.4 0.7 copy.23
  74.1 0.8 unpack.1
  74.9 5.6 %all-to-all-done.3 = f32[32,1,128]{2,1,0:T(1,128)S(1)} async-done(((f32[32,1,128]{2,1,0:T(1,128)}), f32[32,1,128]{2,1,0:T(1,128)S(1)}, u32[]{:S(2)}, u32[]{:S(2)}) %all-to-all-start.3) | async-done | bytes 16416 | tf_op jit(solution)/shard_map/all_to_all | solution.py:281
  80.5 0.1 slice_reduce_fusion
  80.6 0.5 multiply_sqrt_fusion
  (2 shorter events, 0.0 us)
Async XLA Ops:
  69.5 11.0 %all-to-all-start.3 = ((f32[32,1,128]{2,1,0:T(1,128)}), f32[32,1,128]{2,1,0:T(1,128)S(1)}, u32[]{:S(2)}, u32[]{:S(2)}) async-start(f32[32,1,128]{2,1,0:T(1,128)} %broadcast_in_dim.2), calls=%async_computation.3 | async-start | bytes 32768 | tf_op jit(solution)/shard_map/all_to_all | solution.py:281

commit v4 on v3

--- a/solution.py
+++ b/solution.py
@@ -15,7 +15,6 @@
 LIM3, SQ3 = 30, 43
 ROWS3 = 48
 HI = 40
-HIP = 48
 
 
 def pack_kernel(vm, va, ds, mu, inj, ang, fb, tb, g, b, h, rt, st, sl, zd, out, table, line):
@@ -82,11 +81,10 @@
     return high, low
 
 
-def main_kernel(r1, r2, out, tab, split, consts, sides, acc, sums, *bufs):
+def main_kernel(r1, r2, out, tab, split, wide, consts, sides, acc, sums, *bufs):
     for n in range(80):
         b, t = divmod(n, 10)
         m, s = divmod(n, 5)
-        lanes = slice((n % 2) * 128, (n % 2) * 128 + 128)
         for q, (at, row) in enumerate(((DVM, VM2), (DVA, VA2))):
             if s < 2:
                 base = r2[2 * m, row + s : row + s + 1, :]
@@ -94,15 +92,18 @@
                 base = r2[2 * m, row + 2 : row + 3, :] + r2[2 * m + 1, row : row + 1, :]
             else:
                 base = r2[2 * m + 1, row + s - 2 : row + s - 1, :]
-            tab[q * HI + n // 2 : q * HI + n // 2 + 1, lanes] = base + r1[b, at + t : at + t + 1, :]
-        for q, at in ((2, MP), (3, MQ)):
-            tab[q * HI + n // 2 : q * HI + n // 2 + 1, lanes] = r1[b, at + t : at + t + 1, :]
-    high, low = in_two(tab[...])
-    for k in range(2):
-        split[k] = high[:, k * 128 : k * 128 + 128]
-        split[k + 2] = low[:, k * 128 : k * 128 + 128]
-    acc[...] = jnp.zeros((6 * HIP, 256), F32)
+            wide[q, n] = jnp.broadcast_to(base + r1[b, at + t : at + t + 1, :], (8, 128))
+        for q, at in enumerate((MP, MQ)):
+            tab[n % 2, q * HI + n // 2 : q * HI + n // 2 + 1, :] = r1[b, at + t : at + t + 1, :]
+    for half in range(2):
+        high, low = in_two(tab[half])
+        split[half, 0 : 2 * HI, :] = high
+        split[half, 2 * HI : 4 * HI, :] = low
+    acc[...] = jnp.zeros((6 * HI, 256), F32)
     numbers = lax.broadcasted_iota(jnp.int32, (256, 128), 0).astype(F32).astype(BF16)
+    place = lax.broadcasted_iota(jnp.int32, (16, 128), 0)
+    tail = (lax.rem(place, 8) + 32).astype(F32).astype(BF16)
+    upper = (place < 8).astype(F32).astype(BF16) > jnp.zeros((16, 128), BF16)
     for t in range(13):
         for p in range(5):
             k, c = divmod(p * 13 + t, 32)
@@ -112,9 +113,6 @@
     rows_hi = lax.broadcasted_iota(jnp.int32, (HI, 128), 0).astype(F32)
     one, zero = jnp.ones((256, 128), BF16), jnp.zeros((256, 128), BF16)
 
-    def table():
-        return jnp.concatenate([split[k] for k in range(4)], 1)
-
     def across(ref, r):
         return jnp.broadcast_to(ref[r : r + 1, :], (16, 128))
 
@@ -128,15 +126,29 @@
             hi = jnp.floor(index * (1.0 / 256.0))
             ends[2 * e] = hi
             ends[2 * e + 1] = index - hi * 256.0
+            whole = index.astype(jnp.int32)
+            row, lane = lax.shift_right_logical(whole, 7), jnp.bitwise_and(whole, 127)
+            found = [jnp.zeros((8, 128), F32)] * 2
+            for n in range(80):
+                here = row == n
+                for q in range(2):
+                    turned = jnp.take_along_axis(wide[q, n], lane, axis=1, mode="promise_in_bounds")
+                    found[q] = jnp.where(here, turned, found[q])
+            for q in range(2):
+                got[e * 4 + q] = found[q]
             for pair in range(4):
                 weights = jnp.concatenate([hot(ends, e, 2 * pair), hot(ends, e, 2 * pair + 1)], 1)
-                picked = jnp.dot(table(), jnp.concatenate([weights, weights], 0), preferred_element_type=F32)
+                table = jnp.concatenate([split[0], split[1]], 1)
+                picked = jnp.dot(table, weights, preferred_element_type=F32)
                 for half in range(2):
                     r = 2 * pair + half
+                    lanes = slice(half * 128, half * 128 + 128)
                     mask = jnp.broadcast_to(ends[2 * e, r : r + 1, :], (HI, 128)) == rows_hi
-                    for q in range(4):
-                        part = picked[q * HI : q * HI + HI, half * 128 : half * 128 + 128]
-                        got[e * 4 + q, r : r + 1, :] = jnp.sum(jnp.where(mask, part, 0.0), axis=0, keepdims=True)
+                    for q in range(2):
+                        part = (
+                            picked[q * HI : q * HI + HI, lanes] + picked[(q + 2) * HI : (q + 3) * HI, lanes]
+                        )
+                        got[e * 4 + 2 + q, r : r + 1, :] = jnp.sum(jnp.where(mask, part, 0.0), axis=0, keepdims=True)
         g, b, h = consts[2, t], consts[3, t], consts[4, t]
         live, room = sides[0, t], sides[1, t]
         vf, vt = got[0], got[4]
@@ -158,15 +170,15 @@
         for e in range(2):
             for r in range(8):
                 row = across(ends.at[2 * e], r).astype(BF16)
-                mask = numbers[0:HIP, :] == jnp.concatenate([row] * 3, 0)
-                highs, lows = [], []
+                masks = [numbers[0:16] == row, numbers[16:32] == row, tail == row]
                 for k in range(3):
                     high, low = in_two(across(vals.at[e * 3 + k], r))
-                    highs.append(jnp.where(mask, jnp.concatenate([high] * 3, 0), zero[0:HIP]))
-                    lows.append(jnp.where(mask, jnp.concatenate([low] * 3, 0), zero[0:HIP]))
-                rows.append(jnp.concatenate(highs + lows, 0))
+                    mixed = jnp.where(upper, high, low)
+                    five = ((0, high), (1, high), (0, low), (1, low), (2, mixed))
+                    rows += [jnp.where(masks[i], value, zero[0:16]) for i, value in five]
                 cols.append(hot(ends, e, r))
-        rows, cols = jnp.concatenate(rows, 1), jnp.concatenate(cols, 1)
+        rows = jnp.concatenate([jnp.concatenate(rows[15 * i : 15 * i + 15], 0) for i in range(16)], 1)
+        cols = jnp.concatenate(cols, 1)
         acc[...] += lax.dot_general(rows, cols, (((1,), (1,)), ((), ())), preferred_element_type=F32)
 
     even, odd = bufs[:3], bufs[3:]
@@ -192,12 +204,12 @@
     for k in range(3):
         for half in range(2):
             lanes = slice(half * 128, half * 128 + 128)
-            sums[half, k * HIP : k * HIP + HIP, :] = (
-                acc[k * HIP : k * HIP + HIP, lanes] + acc[(k + 3) * HIP : (k + 4) * HIP, lanes]
-            )
+            at = 2 * HI * k
+            sums[half, k * HI : k * HI + 32, :] = acc[at : at + 32, lanes] + acc[at + 32 : at + 64, lanes]
+            sums[half, k * HI + 32 : k * HI + HI, :] = acc[at + 64 : at + 72, lanes] + acc[at + 72 : at + 80, lanes]
     for k in range(3):
         for t in range(10):
-            total = sums[t % 2, pl.ds(k * HIP + t // 2, 8, stride=5), :]
+            total = sums[t % 2, pl.ds(k * HI + t // 2, 8, stride=5), :]
             if k < 2:
                 total = total - r1[:, INJ + k * 10 + t, :]
                 mis_sq = mis_sq + total * total
@@ -212,6 +224,11 @@
     out[:, SQ3, :] = squares
     for r in range(SQ3 + 1, ROWS3):
         out[:, r, :] = jnp.zeros((8, 128), F32)
+
+
+def norms_kernel(r3, out):
+    total = jnp.sum(r3[:, SQ3, :], axis=0, keepdims=True)
+    out[...] = jnp.broadcast_to(total[None], (32, 1, 128))
 
 
 def unpack_kernel(r3, mismatch, dual, limit):
@@ -260,12 +277,13 @@
         out_specs=VM_SPEC,
         in_specs=[VM_SPEC, VM_SPEC],
         scratch_shapes=[
-            pltpu.VMEM((4 * HI, 256), F32),
-            pltpu.VMEM((4, 4 * HI, 128), BF16),
+            pltpu.VMEM((2, 2 * HI, 128), F32),
+            pltpu.VMEM((2, 4 * HI, 128), BF16),
+            pltpu.VMEM((2, 80, 8, 128), F32),
             pltpu.VMEM((5, 13, 8, 128), F32),
             pltpu.VMEM((3, 13, 8, 128), F32),
-            pltpu.VMEM((6 * HIP, 256), F32),
-            pltpu.VMEM((2, 3 * HIP, 128), F32),
+            pltpu.VMEM((6 * HI, 256), F32),
+            pltpu.VMEM((2, 3 * HI, 128), F32),
         ]
         + [
             pltpu.VMEM((4, 8, 128), F32),
@@ -277,7 +295,13 @@
     )(near(r1), near(r2))
     r3 = lax.all_to_all(send3, "br", 0, 0, tiled=True)
     squares = r3[:, SQ3, :]
-    send4 = jnp.broadcast_to(jnp.sum(squares, axis=0)[None, None], (32, 1, 128))
+    send4 = pl.pallas_call(
+        norms_kernel,
+        out_shape=pltpu.VMEM((32, 1, 128), F32),
+        in_specs=[VM_SPEC],
+        out_specs=VM_SPEC,
+        name="norms",
+    )(near(r3))
     r4 = lax.all_to_all(send4, "ctg", 0, 0, tiled=True)
     mismatch, dual, limit = pl.pallas_call(
         unpack_kernel, out_shape=(of((8, 2, 1280)), of((8, 1280)), of((8, 1664))), name="unpack", in_specs=[VM_SPEC]

time: 81.4 us -> 78.7 us (0.967)
  Pallas kernels: 13.3 us -> 11.3 us
    pallas_call x1, Pallas kernels: 11 us -> 8.44 us  [per_device(): pl.pallas_call(main_kernel, out_shape=pltpu.VMEM((8, ROWS3, 128), F32), o...]
where the time goes in v4:
time: 78.7 us; the launch traced here: 78.4 us
  blocking collectives  55.7 us (71%)
  Pallas kernels  11.3 us (14%)
  waiting for transfers between devices  5.62 us (7%)
  starting transfers between devices  3.85 us (5%)
    all_to_all x1, blocking collectives, per_device(): r1 = lax.all_to_all(send1, 'br', 0, 0, tiled=True)  22.7 us
    all_to_all x1, blocking collectives, per_device(): r2 = lax.all_to_all(send2, 'ctg', 0, 0, tiled=True)  19.6 us
    all_to_all x1, blocking collectives, per_device(): r3 = lax.all_to_all(send3, 'br', 0, 0, tiled=True)  13.4 us
    pallas_call x1, Pallas kernels, per_device(): pl.pallas_call(main_kernel, out_shape=pltpu.VMEM((8, ROWS3, 128), F32), o...  8.44 us
    all_to_all x1, waiting for transfers between devices, per_device(): r4 = lax.all_to_all(send4, 'ctg', 0, 0, tiled=True)  5.62 us
    all_to_all x1, starting transfers between devices, per_device(): r4 = lax.all_to_all(send4, 'ctg', 0, 0, tiled=True)  3.85 us
  transfers between devices with their start and end apart: 1, of which 1 were waited for; matrix products, arithmetic and copies ran while one was open for 1% of the time, Pallas kernels for 1%

profile of v4, /device:TPU:1, one launch (start us, length us, event | category | flops | bytes accessed | tf_op | source)
XLA Modules:
  0.0 78.4 jit_solution(13701368939717755809)
XLA Ops:
  0.6 1.4 %pack.1 = f32[8,104,128]{2,1,0:T(8,128)S(1)} custom-call(f32[1,40]{1,0:T(1,128)} %bitcast.16, f32[1,40]{1,0:T(1,128)} %bitcast.17, f32[8,2,1280]{2,1,0:T(2,128)} %ds.1, f32[8,2,1280]{2,1,0:T(2,128)} %mu.1, f32[8,2,1280]{2,1,0:T(2,128)} %inj.1, f32[8,1280]{1,0:T(8,128)} %ang.1, s32[13,128]{1,0:T(8,128)} %bitcast.10, s32[13,128]{1,0:T(8,128)} %bitcast.11, ...), custom_call_target="tpu_custom_call" | custom-call | tf_op jit(solution)/shard_map/pack/pallas_call | solution.py:257
  2.0 22.7 %all_to_all.20.part.r1 = f32[8,104,128]{2,1,0:T(8,128)S(1)} all-to-all(f32[8,104,128]{2,1,0:T(8,128)S(1)} %pack.1), channel_id=1, replica_groups=mesh['ctg'=32,'br'=8] {'br'}, dimensions={0} | all-to-all | bytes 851968 | tf_op jit(solution)/shard_map/all_to_all | solution.py:264
  24.7 0.1 spread.1
  24.8 19.6 %all_to_all.21.r2 = f32[32,24,128]{2,1,0:T(8,128)S(1)} all-to-all(f32[32,24,128]{2,1,0:T(8,128)S(1)} %spread.1), channel_id=1, replica_groups=mesh['ctg'=32,'br'=8] {'ctg'}, dimensions={0} | all-to-all | bytes 786432 | tf_op jit(solution)/shard_map/all_to_all | solution.py:273
  44.4 8.4 %main.1 = f32[8,48,128]{2,1,0:T(8,128)S(1)} custom-call(f32[8,104,128]{2,1,0:T(8,128)S(1)} %all_to_all.20.part.r1, f32[32,24,128]{2,1,0:T(8,128)S(1)} %all_to_all.21.r2), custom_call_target="tpu_custom_call" | custom-call | tf_op jit(solution)/shard_map/main/pallas_call | solution.py:274
  52.9 13.4 %all_to_all.22.r3 = f32[8,48,128]{2,1,0:T(8,128)S(1)} all-to-all(f32[8,48,128]{2,1,0:T(8,128)S(1)} %main.1), channel_id=1, replica_groups=mesh['ctg'=32,'br'=8] {'br'}, dimensions={0} | all-to-all | bytes 393216 | tf_op jit(solution)/shard_map/all_to_all | solution.py:296
  66.3 0.6 norms.1
  66.9 3.9 %all-to-all-start.3 = ((f32[32,1,128]{2,1,0:T(1,128)}), f32[32,1,128]{2,1,0:T(1,128)S(1)}, u32[]{:S(2)}, u32[]{:S(2)}) async-start(f32[32,1,128]{2,1,0:T(1,128)} %norms.1), calls=%async_computation.3 | async-start | bytes 32768 | tf_op jit(solution)/shard_map/all_to_all | solution.py:305
  70.8 0.7 copy.20
  71.4 0.8 unpack.1
  72.2 5.6 %all-to-all-done.3 = f32[32,1,128]{2,1,0:T(1,128)S(1)} async-done(((f32[32,1,128]{2,1,0:T(1,128)}), f32[32,1,128]{2,1,0:T(1,128)S(1)}, u32[]{:S(2)}, u32[]{:S(2)}) %all-to-all-start.3) | async-done | bytes 16416 | tf_op jit(solution)/shard_map/all_to_all | solution.py:305
  77.8 0.1 slice_reduce_fusion
  77.9 0.5 multiply_sqrt_fusion
  (2 shorter events, 0.0 us)
Async XLA Ops:
  66.9 10.9 %all-to-all-start.3 = ((f32[32,1,128]{2,1,0:T(1,128)}), f32[32,1,128]{2,1,0:T(1,128)S(1)}, u32[]{:S(2)}, u32[]{:S(2)}) async-start(f32[32,1,128]{2,1,0:T(1,128)} %norms.1), calls=%async_computation.3 | async-start | bytes 32768 | tf_op jit(solution)/shard_map/all_to_all | solution.py:305

commit v5 on v4

--- a/solution.py
+++ b/solution.py
@@ -231,7 +231,7 @@
     out[...] = jnp.broadcast_to(total[None], (32, 1, 128))
 
 
-def unpack_kernel(r3, mismatch, dual, limit):
+def final_kernel(r3, r4, mismatch, dual, limit, norms, total):
     for t in range(10):
         lanes = slice(t * 128, t * 128 + 128)
         for k in range(2):
@@ -239,6 +239,9 @@
         dual[:, lanes] = r3[:, 20 + t, :]
     for t in range(13):
         limit[:, t * 128 : t * 128 + 128] = r3[:, LIM3 + t, :]
+    norms[...] = jnp.sqrt(jnp.transpose(r3[:, SQ3, :]))[0:4]
+    whole = jnp.sum(r4[:, 0, :], axis=0, keepdims=True)
+    total[...] = jnp.sqrt(whole * (1.0 / 256.0))[:, 0:4]
 
 
 VM_SPEC = pl.BlockSpec(memory_space=pltpu.VMEM)
@@ -294,7 +297,6 @@
         name="main",
     )(near(r1), near(r2))
     r3 = lax.all_to_all(send3, "br", 0, 0, tiled=True)
-    squares = r3[:, SQ3, :]
     send4 = pl.pallas_call(
         norms_kernel,
         out_shape=pltpu.VMEM((32, 1, 128), F32),
@@ -303,11 +305,13 @@
         name="norms",
     )(near(r3))
     r4 = lax.all_to_all(send4, "ctg", 0, 0, tiled=True)
-    mismatch, dual, limit = pl.pallas_call(
-        unpack_kernel, out_shape=(of((8, 2, 1280)), of((8, 1280)), of((8, 1664))), name="unpack", in_specs=[VM_SPEC]
-    )(near(r3))
-    total = jnp.sqrt(jnp.sum(r4[:, 0, 0:4], axis=0) / 256.0)
-    return mismatch, dual, limit, jnp.sqrt(squares[:, 0:4]), total
+    mismatch, dual, limit, norms, total = pl.pallas_call(
+        final_kernel,
+        out_shape=(of((8, 2, 1280)), of((8, 1280)), of((8, 1664)), of((4, 8)), of((1, 4))),
+        in_specs=[VM_SPEC, VM_SPEC],
+        name="final",
+    )(near(r3), near(r4))
+    return mismatch, dual, limit, norms.T, total.reshape(4)
 
 
 def solution(mesh):

time: 78.7 us -> 77.9 us (0.990)
  blocking collectives: 55.7 us -> 66.2 us
  waiting for transfers between devices: 5.62 us -> 0 us
  starting transfers between devices: 3.85 us -> 0 us
    all_to_all x0 -> x1, blocking collectives: none -> 10.5 us  [per_device(): r4 = lax.all_to_all(send4, 'ctg', 0, 0, tiled=True)]
    all_to_all x1 -> x0, waiting for transfers between devices: 5.62 us -> none  [per_device(): r4 = lax.all_to_all(send4, 'ctg', 0, 0, tiled=True)]
    all_to_all x1 -> x0, starting transfers between devices: 3.85 us -> none  [per_device(): r4 = lax.all_to_all(send4, 'ctg', 0, 0, tiled=True)]
  transfers between devices with their start and end apart: 1 -> 0, of which waited for: 1 -> 0; matrix products, arithmetic and copies ran while one was open for 1% -> 0% of each run, Pallas kernels for 1% -> 0%
where the time goes in v5:
time: 77.9 us; the launch traced here: 77.6 us
  blocking collectives  66.2 us (85%)
  Pallas kernels  10.7 us (14%)
    all_to_all x1, blocking collectives, per_device(): r1 = lax.all_to_all(send1, 'br', 0, 0, tiled=True)  22.7 us
    all_to_all x1, blocking collectives, per_device(): r2 = lax.all_to_all(send2, 'ctg', 0, 0, tiled=True)  19.6 us
    all_to_all x1, blocking collectives, per_device(): r3 = lax.all_to_all(send3, 'br', 0, 0, tiled=True)  13.4 us
    all_to_all x1, blocking collectives, per_device(): r4 = lax.all_to_all(send4, 'ctg', 0, 0, tiled=True)  10.5 us
    pallas_call x1, Pallas kernels, per_device(): pl.pallas_call(main_kernel, out_shape=pltpu.VMEM((8, ROWS3, 128), F32), o...  8.44 us

profile of v5, /device:TPU:1, one launch (start us, length us, event | category | flops | bytes accessed | tf_op | source)
XLA Modules:
  0.0 77.6 jit_solution(4508539668381542787)
XLA Ops:
  0.6 1.4 %pack.1 = f32[8,104,128]{2,1,0:T(8,128)S(1)} custom-call(f32[1,40]{1,0:T(1,128)} %bitcast.16, f32[1,40]{1,0:T(1,128)} %bitcast.17, f32[8,2,1280]{2,1,0:T(2,128)} %ds.1, f32[8,2,1280]{2,1,0:T(2,128)} %mu.1, f32[8,2,1280]{2,1,0:T(2,128)} %inj.1, f32[8,1280]{1,0:T(8,128)} %ang.1, s32[13,128]{1,0:T(8,128)} %bitcast.10, s32[13,128]{1,0:T(8,128)} %bitcast.11, ...), custom_call_target="tpu_custom_call" | custom-call | tf_op jit(solution)/shard_map/pack/pallas_call | solution.py:260
  2.0 22.7 %all_to_all.20.part.r1 = f32[8,104,128]{2,1,0:T(8,128)S(1)} all-to-all(f32[8,104,128]{2,1,0:T(8,128)S(1)} %pack.1), channel_id=1, replica_groups=mesh['ctg'=32,'br'=8] {'br'}, dimensions={0} | all-to-all | bytes 851968 | tf_op jit(solution)/shard_map/all_to_all | solution.py:267
  24.7 0.1 spread.1
  24.8 19.6 %all_to_all.21.r2 = f32[32,24,128]{2,1,0:T(8,128)S(1)} all-to-all(f32[32,24,128]{2,1,0:T(8,128)S(1)} %spread.1), channel_id=1, replica_groups=mesh['ctg'=32,'br'=8] {'ctg'}, dimensions={0} | all-to-all | bytes 786432 | tf_op jit(solution)/shard_map/all_to_all | solution.py:276
  44.4 8.4 %main.1 = f32[8,48,128]{2,1,0:T(8,128)S(1)} custom-call(f32[8,104,128]{2,1,0:T(8,128)S(1)} %all_to_all.20.part.r1, f32[32,24,128]{2,1,0:T(8,128)S(1)} %all_to_all.21.r2), custom_call_target="tpu_custom_call" | custom-call | tf_op jit(solution)/shard_map/main/pallas_call | solution.py:277
  52.9 13.4 %all_to_all.22.r3 = f32[8,48,128]{2,1,0:T(8,128)S(1)} all-to-all(f32[8,48,128]{2,1,0:T(8,128)S(1)} %main.1), channel_id=1, replica_groups=mesh['ctg'=32,'br'=8] {'br'}, dimensions={0} | all-to-all | bytes 393216 | tf_op jit(solution)/shard_map/all_to_all | solution.py:299
  66.3 10.5 %all_to_all.23.r4 = f32[32,1,128]{2,1,0:T(1,128)S(1)} all-to-all(f32[32,1,128]{2,1,0:T(1,128)S(1)} %norms.1), channel_id=1, replica_groups=mesh['ctg'=32,'br'=8] {'ctg'}, dimensions={0} | all-to-all | bytes 32768 | tf_op jit(solution)/shard_map/all_to_all | solution.py:307
  76.8 0.8 final.1
  (1 shorter events, 0.0 us)

commit v6 on v5

--- a/solution.py
+++ b/solution.py
@@ -128,12 +128,19 @@
             ends[2 * e + 1] = index - hi * 256.0
             whole = index.astype(jnp.int32)
             row, lane = lax.shift_right_logical(whole, 7), jnp.bitwise_and(whole, 127)
+            bits = [jnp.bitwise_and(row, 1 << i) != 0 for i in range(3)]
+            group = lax.shift_right_logical(row, 3)
             found = [jnp.zeros((8, 128), F32)] * 2
-            for n in range(80):
-                here = row == n
+            for n in range(10):
+                here = group == n
                 for q in range(2):
-                    turned = jnp.take_along_axis(wide[q, n], lane, axis=1, mode="promise_in_bounds")
-                    found[q] = jnp.where(here, turned, found[q])
+                    level = [
+                        jnp.take_along_axis(wide[q, 8 * n + i], lane, axis=1, mode="promise_in_bounds")
+                        for i in range(8)
+                    ]
+                    for bit in bits:
+                        level = [jnp.where(bit, y, x) for x, y in zip(level[::2], level[1::2])]
+                    found[q] = jnp.where(here, level[0], found[q])
             for q in range(2):
                 got[e * 4 + q] = found[q]
             for pair in range(4):
@@ -143,12 +150,14 @@
                 for half in range(2):
                     r = 2 * pair + half
                     lanes = slice(half * 128, half * 128 + 128)
-                    mask = jnp.broadcast_to(ends[2 * e, r : r + 1, :], (HI, 128)) == rows_hi
+                    wanted = jnp.broadcast_to(ends[2 * e, r : r + 1, :], (8, 128))
                     for q in range(2):
-                        part = (
-                            picked[q * HI : q * HI + HI, lanes] + picked[(q + 2) * HI : (q + 3) * HI, lanes]
-                        )
-                        got[e * 4 + 2 + q, r : r + 1, :] = jnp.sum(jnp.where(mask, part, 0.0), axis=0, keepdims=True)
+                        kept = jnp.zeros((8, 128), F32)
+                        for i in range(5):
+                            at = q * HI + 8 * i
+                            part = picked[at : at + 8, lanes] + picked[at + 2 * HI : at + 2 * HI + 8, lanes]
+                            kept = jnp.where(wanted == rows_hi[8 * i : 8 * i + 8], part, kept)
+                        got[e * 4 + 2 + q, r : r + 1, :] = jnp.sum(kept, axis=0, keepdims=True)
         g, b, h = consts[2, t], consts[3, t], consts[4, t]
         live, room = sides[0, t], sides[1, t]
         vf, vt = got[0], got[4]

time: 77.9 us -> 77.8 us (level)
  no operation moved by 1% of the time
where the time goes in v6:
time: 77.8 us; the launch traced here: 77.5 us
  blocking collectives  66.2 us (85%)
  Pallas kernels  10.6 us (14%)
    all_to_all x1, blocking collectives, per_device(): r1 = lax.all_to_all(send1, 'br', 0, 0, tiled=True)  22.7 us
    all_to_all x1, blocking collectives, per_device(): r2 = lax.all_to_all(send2, 'ctg', 0, 0, tiled=True)  19.6 us
    all_to_all x1, blocking collectives, per_device(): r3 = lax.all_to_all(send3, 'br', 0, 0, tiled=True)  13.4 us
    all_to_all x1, blocking collectives, per_device(): r4 = lax.all_to_all(send4, 'ctg', 0, 0, tiled=True)  10.5 us
    pallas_call x1, Pallas kernels, per_device(): pl.pallas_call(main_kernel, out_shape=pltpu.VMEM((8, ROWS3, 128), F32), o...  8.33 us

profile of v6, /device:TPU:1, one launch (start us, length us, event | category | flops | bytes accessed | tf_op | source)
XLA Modules:
  0.0 77.5 jit_solution(1938029354151160116)
XLA Ops:
  0.6 1.4 %pack.1 = f32[8,104,128]{2,1,0:T(8,128)S(1)} custom-call(f32[1,40]{1,0:T(1,128)} %bitcast.16, f32[1,40]{1,0:T(1,128)} %bitcast.17, f32[8,2,1280]{2,1,0:T(2,128)} %ds.1, f32[8,2,1280]{2,1,0:T(2,128)} %mu.1, f32[8,2,1280]{2,1,0:T(2,128)} %inj.1, f32[8,1280]{1,0:T(8,128)} %ang.1, s32[13,128]{1,0:T(8,128)} %bitcast.10, s32[13,128]{1,0:T(8,128)} %bitcast.11, ...), custom_call_target="tpu_custom_call" | custom-call | tf_op jit(solution)/shard_map/pack/pallas_call | solution.py:269
  2.0 22.7 %all_to_all.20.part.r1 = f32[8,104,128]{2,1,0:T(8,128)S(1)} all-to-all(f32[8,104,128]{2,1,0:T(8,128)S(1)} %pack.1), channel_id=1, replica_groups=mesh['ctg'=32,'br'=8] {'br'}, dimensions={0} | all-to-all | bytes 851968 | tf_op jit(solution)/shard_map/all_to_all | solution.py:276
  24.7 0.1 spread.1
  24.8 19.6 %all_to_all.21.r2 = f32[32,24,128]{2,1,0:T(8,128)S(1)} all-to-all(f32[32,24,128]{2,1,0:T(8,128)S(1)} %spread.1), channel_id=1, replica_groups=mesh['ctg'=32,'br'=8] {'ctg'}, dimensions={0} | all-to-all | bytes 786432 | tf_op jit(solution)/shard_map/all_to_all | solution.py:285
  44.4 8.3 %main.1 = f32[8,48,128]{2,1,0:T(8,128)S(1)} custom-call(f32[8,104,128]{2,1,0:T(8,128)S(1)} %all_to_all.20.part.r1, f32[32,24,128]{2,1,0:T(8,128)S(1)} %all_to_all.21.r2), custom_call_target="tpu_custom_call" | custom-call | tf_op jit(solution)/shard_map/main/pallas_call | solution.py:286
  52.8 13.4 %all_to_all.22.r3 = f32[8,48,128]{2,1,0:T(8,128)S(1)} all-to-all(f32[8,48,128]{2,1,0:T(8,128)S(1)} %main.1), channel_id=1, replica_groups=mesh['ctg'=32,'br'=8] {'br'}, dimensions={0} | all-to-all | bytes 393216 | tf_op jit(solution)/shard_map/all_to_all | solution.py:308
  66.2 10.5 %all_to_all.23.r4 = f32[32,1,128]{2,1,0:T(1,128)S(1)} all-to-all(f32[32,1,128]{2,1,0:T(1,128)S(1)} %norms.1), channel_id=1, replica_groups=mesh['ctg'=32,'br'=8] {'ctg'}, dimensions={0} | all-to-all | bytes 32768 | tf_op jit(solution)/shard_map/all_to_all | solution.py:316
  76.7 0.8 final.1
  (1 shorter events, 0.0 us)

commit v7 on v6

--- a/solution.py
+++ b/solution.py
@@ -172,7 +172,9 @@
         fd = live * u * (got[2] * (gs - bc) - got[3] * (gc + bs) + got[6] * (gs + bc) + got[7] * (gc - bs))
         sides[2, t] = live * (pf * pf + qf * qf + room)
         for k, value in enumerate((pf, qf, fd, pt, qt, -fd)):
-            vals[k] = value
+            high = value.astype(BF16).astype(F32)
+            vals[k] = high
+            vals[k + 6] = value - high
 
     def scatter(ends, got, vals):
         rows, cols = [], []
@@ -181,7 +183,8 @@
                 row = across(ends.at[2 * e], r).astype(BF16)
                 masks = [numbers[0:16] == row, numbers[16:32] == row, tail == row]
                 for k in range(3):
-                    high, low = in_two(across(vals.at[e * 3 + k], r))
+                    high = across(vals.at[e * 3 + k], r).astype(BF16)
+                    low = across(vals.at[e * 3 + k + 6], r).astype(BF16)
                     mixed = jnp.where(upper, high, low)
                     five = ((0, high), (1, high), (0, low), (1, low), (2, mixed))
                     rows += [jnp.where(masks[i], value, zero[0:16]) for i, value in five]
@@ -300,7 +303,7 @@
         + [
             pltpu.VMEM((4, 8, 128), F32),
             pltpu.VMEM((8, 8, 128), F32),
-            pltpu.VMEM((6, 8, 128), F32),
+            pltpu.VMEM((12, 8, 128), F32),
         ]
         * 2,
         name="main",

time: 77.8 us -> 77.8 us (level)
  no operation moved by 1% of the time
where the time goes in v7:
time: 77.8 us; the launch traced here: 77.5 us
  blocking collectives  66.2 us (85%)
  Pallas kernels  10.6 us (14%)
    all_to_all x1, blocking collectives, per_device(): r1 = lax.all_to_all(send1, 'br', 0, 0, tiled=True)  22.7 us
    all_to_all x1, blocking collectives, per_device(): r2 = lax.all_to_all(send2, 'ctg', 0, 0, tiled=True)  19.6 us
    all_to_all x1, blocking collectives, per_device(): r3 = lax.all_to_all(send3, 'br', 0, 0, tiled=True)  13.4 us
    all_to_all x1, blocking collectives, per_device(): r4 = lax.all_to_all(send4, 'ctg', 0, 0, tiled=True)  10.5 us
    pallas_call x1, Pallas kernels, per_device(): pl.pallas_call(main_kernel, out_shape=pltpu.VMEM((8, ROWS3, 128), F32), o...  8.34 us

profile of v7, /device:TPU:1, one launch (start us, length us, event | category | flops | bytes accessed | tf_op | source)
XLA Modules:
  0.0 77.5 jit_solution(15182265806152281859)
XLA Ops:
  0.6 1.4 %pack.1 = f32[8,104,128]{2,1,0:T(8,128)S(1)} custom-call(f32[1,40]{1,0:T(1,128)} %bitcast.16, f32[1,40]{1,0:T(1,128)} %bitcast.17, f32[8,2,1280]{2,1,0:T(2,128)} %ds.1, f32[8,2,1280]{2,1,0:T(2,128)} %mu.1, f32[8,2,1280]{2,1,0:T(2,128)} %inj.1, f32[8,1280]{1,0:T(8,128)} %ang.1, s32[13,128]{1,0:T(8,128)} %bitcast.10, s32[13,128]{1,0:T(8,128)} %bitcast.11, ...), custom_call_target="tpu_custom_call" | custom-call | tf_op jit(solution)/shard_map/pack/pallas_call | solution.py:272
  2.0 22.7 %all_to_all.20.part.r1 = f32[8,104,128]{2,1,0:T(8,128)S(1)} all-to-all(f32[8,104,128]{2,1,0:T(8,128)S(1)} %pack.1), channel_id=1, replica_groups=mesh['ctg'=32,'br'=8] {'br'}, dimensions={0} | all-to-all | bytes 851968 | tf_op jit(solution)/shard_map/all_to_all | solution.py:279
  24.7 0.1 spread.1
  24.8 19.6 %all_to_all.21.r2 = f32[32,24,128]{2,1,0:T(8,128)S(1)} all-to-all(f32[32,24,128]{2,1,0:T(8,128)S(1)} %spread.1), channel_id=1, replica_groups=mesh['ctg'=32,'br'=8] {'ctg'}, dimensions={0} | all-to-all | bytes 786432 | tf_op jit(solution)/shard_map/all_to_all | solution.py:288
  44.4 8.3 %main.1 = f32[8,48,128]{2,1,0:T(8,128)S(1)} custom-call(f32[8,104,128]{2,1,0:T(8,128)S(1)} %all_to_all.20.part.r1, f32[32,24,128]{2,1,0:T(8,128)S(1)} %all_to_all.21.r2), custom_call_target="tpu_custom_call" | custom-call | tf_op jit(solution)/shard_map/main/pallas_call | solution.py:289
  52.8 13.4 %all_to_all.22.r3 = f32[8,48,128]{2,1,0:T(8,128)S(1)} all-to-all(f32[8,48,128]{2,1,0:T(8,128)S(1)} %main.1), channel_id=1, replica_groups=mesh['ctg'=32,'br'=8] {'br'}, dimensions={0} | all-to-all | bytes 393216 | tf_op jit(solution)/shard_map/all_to_all | solution.py:311
  66.2 10.5 %all_to_all.23.r4 = f32[32,1,128]{2,1,0:T(1,128)S(1)} all-to-all(f32[32,1,128]{2,1,0:T(1,128)S(1)} %norms.1), channel_id=1, replica_groups=mesh['ctg'=32,'br'=8] {'ctg'}, dimensions={0} | all-to-all | bytes 32768 | tf_op jit(solution)/shard_map/all_to_all | solution.py:319
  76.7 0.8 final.1
  (1 shorter events, 0.0 us)
